TPU v7x, 512 devices: a whole 4x4x16 slice. The times are simulated.
512 devices in a mesh: tm: 32 (over z, core), batch: 16 (over x, y).
Axes of the slice: x: 4, y: 4, z: 16, core: 2. Of those that a mesh axis runs over, the one named last changes fastest.
Arguments:
- rewards: float32 [2048, 32768], P('batch', 'tm'), may hold values from -0.12 to 0.12
- values: float32 [2048, 32768], P('batch', 'tm'), may hold values from -3 to 3
- episode_ends: int32 [2048, 32768], P('batch', 'tm'), may hold values 0 or 1
- lengths: int32 [2048], P('batch'), may hold values from 8192 to 32768
- groups: int32 [2048], P('batch'), may hold values from 0 to 127, as said below
Outputs:
- advantages: float32 [2048, 32768], P('batch', 'tm')
- grouped_advantages: float32 [2048, 32768], P('batch', 'tm')
- grouped_returns: float32 [2048, 32768], P('batch', 'tm')
Inputs may be any that keep to these rules, and one draw needn't show every extreme that they name: `groups`: every group has exactly one rollout in each aligned block of 128 rollouts.
All inputs are finite; a program needn't handle non-finite values. No bound on the sum of `episode_ends` on one device may be relied on, other than what follows from the above.
Results may differ from a plain program's by a relative error of at most 0.0003.
Values sent between devices are 32-bit elements; how exact they have to be, the bound alone decides.
A program may use at most 64 MiB of HBM per device.

v0:
```python
import jax
import jax.numpy as jnp
from jax import lax
from jax.sharding import Mesh
from jax.sharding import PartitionSpec as P

GROUP = 16
TM = ("tm_0", "tm_1")
BATCH = ("batch_0", "batch_1")
TM_BATCH = ("tm_0", "tm_1", "batch_0", "batch_1")


GAMMA_RATE = 0.9995
ALPHA_RATE = 0.05
EPSILON = 1e-06


def passed_along(value, axis, by):
    size = lax.axis_size(axis)
    pairs = [(i, i + by) for i in range(size) if 0 <= i + by < size]
    return lax.ppermute(value, axis, pairs)


def copy_for_each(value, axis):
    size = lax.axis_size(axis)
    return lax.all_to_all(
        jnp.broadcast_to(value[None], (size, *value.shape)), axis, 0, 0, tiled=True
    )


def gathered_once(value, axis):
    leaves = jax.tree.leaves(value)
    sequence = sorted(range(len(leaves)), key=lambda k: -leaves[k].size)
    width = (1, *leaves[sequence[0]].shape)[-1]
    lines = [
        jnp.pad(leaves[k].reshape(-1), (0, -leaves[k].size % width)).reshape(-1, width)
        for k in sequence
    ]
    both, at, found = (copy_for_each(jnp.concatenate(lines), axis), 0, {})
    for k, line in zip(sequence, lines):
        piece = both[:, at : at + len(line)].reshape(len(both), -1)
        found[k] = piece[:, : leaves[k].size].reshape(-1, *leaves[k].shape)
        at += len(line)
    numbers = iter(range(len(leaves)))
    return jax.tree.map(lambda _: found[next(numbers)], value)


def folded_in_pairs(pieces, combine):
    while len(jax.tree.leaves(pieces)[0]) > 1:
        pieces = jax.vmap(combine)(
            *(jax.tree.map(lambda part: part[side::2], pieces) for side in (0, 1))
        )
    return jax.tree.map(lambda part: part[0], pieces)


def carried_in(value, axis, combine, identity):
    size, mine = (lax.axis_size(axis), lax.axis_index(axis))
    passed = jnp.arange(size) > mine

    def kept(part, zero, own):
        part = jnp.where(
            passed.reshape(-1, *(1 for _ in own.shape)), part, jnp.asarray(zero, own.dtype)
        )
        return part[::-1]

    pieces = gathered_once(value, axis)
    return folded_in_pairs(jax.tree.map(kept, pieces, identity, value), combine)


def over_axes(value, axes):
    for axis in axes:
        value = lax.psum(value, axis)
    return value


def compose(earlier, later):
    return (
        later[0] * earlier[0],
        later[1] + later[0] * earlier[1],
        later[2] * earlier[2],
        later[3] + later[2] * earlier[3],
    )


def chain_terms(rewards, values, episode_ends, lengths, next_first, start):
    positions = start + lax.broadcasted_iota(jnp.int32, rewards.shape, 1)
    limit = lengths[:, None]
    inside = positions < limit
    final = (episode_ends == 1) | (positions == limit - 1)
    carry_on = jnp.where(inside & jnp.logical_not(final), 1.0, 0.0).astype(jnp.float32)
    value_next = jnp.concatenate([values[:, 1:], next_first], axis=1)
    reward_in = jnp.where(inside, rewards, 0.0)
    delta = jnp.where(inside, reward_in + GAMMA_RATE * carry_on * value_next - values, 0.0)
    lambdas = 1.0 - 1.0 / (ALPHA_RATE * lengths.astype(jnp.float32))
    return (carry_on, reward_in, GAMMA_RATE * lambdas, delta)


def rate_power(steps, log_rate, negative):
    magnitude = jnp.exp(steps * log_rate)
    parity = steps - 2.0 * jnp.floor(steps * 0.5)
    return jnp.where(negative & (parity > 0.5), -magnitude, magnitude)


def block_chain(carry_on, first_in, second_in, second_rate):
    height, span = carry_on.shape
    width = min(span, 128)
    count = span // width
    index = lax.broadcasted_iota(jnp.int32, (width, width), 0)
    other = lax.broadcasted_iota(jnp.int32, (width, width), 1)
    lower = (index < other).astype(jnp.float32)
    upper = other >= index
    distance = jnp.maximum(other - index, 0).astype(jnp.float32)
    lanes = lax.broadcasted_iota(jnp.int32, (1, width), 1).astype(jnp.float32)
    rates = (jnp.full((height,), GAMMA_RATE, jnp.float32), second_rate)
    log_rates = tuple((jnp.log(jnp.maximum(jnp.abs(rate), 1e-30))[:, None] for rate in rates))
    negatives = tuple(((rate < 0.0)[:, None] for rate in rates))
    inputs = (first_in, second_in)
    carry_mult = [jnp.ones((height,), jnp.float32), jnp.ones((height,), jnp.float32)]
    carry_add = [jnp.zeros((height,), jnp.float32), jnp.zeros((height,), jnp.float32)]
    mult_parts = [[], []]
    add_parts = [[], []]
    for block in reversed(range(count)):
        low = block * width
        continued = carry_on[:, low : low + width]
        breaks = 1.0 - continued
        before = jnp.dot(breaks, lower, precision=lax.Precision.HIGHEST)
        total = jnp.sum(breaks, 1, keepdims=True)
        same = (before[:, :, None] == before[:, None, :]) & upper[None, :, :]
        open_tail = before == total
        tail_steps = width - lanes
        for which in range(2):
            weight = jnp.where(
                same,
                rate_power(
                    distance[None, :, :], log_rates[which][:, :, None], negatives[which][:, :, None]
                ),
                0.0,
            )
            piece = inputs[which][:, low : low + width]
            local = jnp.einsum("bts,bs->bt", weight, piece, precision=lax.Precision.HIGHEST)
            tail = jnp.where(
                open_tail, rate_power(tail_steps, log_rates[which], negatives[which]), 0.0
            )
            mult_pos = tail * carry_mult[which][:, None]
            add_pos = local + tail * carry_add[which][:, None]
            mult_parts[which].insert(0, mult_pos)
            add_parts[which].insert(0, add_pos)
            carry_mult[which] = mult_pos[:, 0]
            carry_add[which] = add_pos[:, 0]
    joined = [
        jnp.concatenate(parts, 1)
        for parts in (mult_parts[0], add_parts[0], mult_parts[1], add_parts[1])
    ]
    return tuple(joined)


def regroup_source(groups, members):
    height = groups.shape[0]
    per_dest = height // GROUP
    index_row = lax.broadcasted_iota(jnp.int32, (height, height), 0)
    index_col = lax.broadcasted_iota(jnp.int32, (height, height), 1)
    same_earlier = (groups[:, None] == groups[None, :]) & (index_col < index_row)
    rank = jnp.sum(same_earlier.astype(jnp.int32), 1)
    slot = groups // per_dest * (per_dest * members) + groups % per_dest * members + rank
    return jnp.zeros((height,), jnp.int32).at[slot].set(jnp.arange(height, dtype=jnp.int32))


def on_device(rewards, values, episode_ends, lengths, groups):
    height, span = rewards.shape
    start = lax.axis_index(TM) * span
    next_first = passed_along(values[:, :1], TM, -1)
    carry_on, reward_in, second_rate, delta = chain_terms(
        rewards, values, episode_ends, lengths, next_first, start
    )
    scanned = block_chain(carry_on, reward_in, delta, second_rate)
    summary = tuple((item[:, 0] for item in scanned))
    ones = jnp.ones((height,), jnp.float32)
    zeros = jnp.zeros((height,), jnp.float32)
    incoming = carried_in(summary, TM, compose, (ones, zeros, ones, zeros))
    returns = scanned[1] + scanned[0] * incoming[1][:, None]
    advantages = scanned[3] + scanned[2] * incoming[3][:, None]
    batch_count = lax.axis_size(BATCH)
    members = GROUP // batch_count
    per_dest = height // GROUP
    source_of = regroup_source(groups, members)
    counts_here = jnp.clip(lengths - start, 0, span).astype(jnp.float32)
    group_total = height * batch_count // GROUP
    onehot = (groups[:, None] == jnp.arange(group_total, dtype=jnp.int32)[None, :]).astype(
        jnp.float32
    )
    totals = (
        over_axes(jnp.dot(counts_here, onehot, precision=lax.Precision.HIGHEST), TM_BATCH),
        over_axes(
            jnp.dot(jnp.sum(advantages, 1), onehot, precision=lax.Precision.HIGHEST), TM_BATCH
        ),
        over_axes(
            jnp.dot(jnp.sum(advantages * advantages, 1), onehot, precision=lax.Precision.HIGHEST),
            TM_BATCH,
        ),
    )
    group_mean = totals[1] / totals[0]
    group_var = totals[2] / totals[0] - group_mean * group_mean
    row_mean = jnp.dot(onehot, group_mean, precision=lax.Precision.HIGHEST)
    row_var = jnp.dot(onehot, group_var, precision=lax.Precision.HIGHEST)
    positions = start + lax.broadcasted_iota(jnp.int32, (height, span), 1)
    inside = positions < lengths[:, None]
    normalized = jnp.where(
        inside, (advantages - row_mean[:, None]) / jnp.sqrt(row_var[:, None] + EPSILON), 0.0
    )
    norm_buffer = normalized[source_of].reshape(batch_count, per_dest, members, span)
    ret_buffer = returns[source_of].reshape(batch_count, per_dest, members, span)
    received = (
        lax.all_to_all(norm_buffer, BATCH, split_axis=0, concat_axis=2, tiled=True),
        lax.all_to_all(ret_buffer, BATCH, split_axis=0, concat_axis=2, tiled=True),
    )
    grouped_adv = received[0].reshape(height, span)
    grouped_ret = received[1].reshape(height, span)
    return (advantages, grouped_adv, grouped_ret)


def solution(mesh):
    finer = Mesh(mesh.devices.reshape(16, 2, 4, 4), ("tm_0", "tm_1", "batch_0", "batch_1"))
    return jax.shard_map(
        on_device,
        mesh=finer,
        in_specs=(P(BATCH, TM), P(BATCH, TM), P(BATCH, TM), P(BATCH), P(BATCH)),
        out_specs=(P(BATCH, TM), P(BATCH, TM), P(BATCH, TM)),
        check_vma=False,
    )
```

profile of v0, /device:TPU:32, one launch (start us, length us, event | category | flops | bytes accessed | tf_op | source)
XLA Modules:
  0.0 209.2 jit_solution(514335095807465705)
XLA Ops:
  0.7 1.2 copy.98
  1.9 1.9 collective-permute-start
  10.3 1.1 select_multiply_fusion.1
  11.5 1.1 select_multiply_fusion.3
  12.7 1.1 select_multiply_fusion.5
  13.9 1.1 select_multiply_fusion.7
  15.1 1.1 select_multiply_fusion.9
  16.4 1.1 select_multiply_fusion.11
  17.6 32.4 %multiply_reduce_fusion.8 = (f32[128,128]{1,0:T(8,128)S(1)}, f32[128,128]{1,0:T(8,128)S(1)}, f32[128,128]{1,0:T(8,128)S(1)}, f32[128,128]{1,0:T(8,128)S(1)}, f32...) fusion(f32[128,128]{1,0:T(8,128)S(1)} %copy.223, f32[128,128]{1,0:T(8,128)S(1)} %copy.113, ...), kind=kLoop, calls=%fused_computation.12 | loop fusion | flops 81674240 | bytes 1475200
  54.0 6.7 %multiply_reduce_fusion.15 = f32[128,128]{1,0:T(8,128)S(1)} fusion(f32[128,128]{1,0:T(8,128)S(1)} %copy.216, f32[128]{0:T(128)S(1)} %maximum_log_fusion, f32[128,128]{1,0:T(8,128)S(1)} %maximum_convert_fusion, f32[128,128]{1,0:T(8,128)S(1)} %copy.95, pred[128,128]{1,0:T(8,128)(4,1)S(1)} %get-tuple-element.157, pred[128,128]{1,0:T(8,128)(4,1)S(1)} %get-tuple-element.158, ...), kind=kLoop, calls=%fused_computation.19 | loop fusion | flops 18857984 | bytes 295552
  61.4 35.4 %multiply_reduce_fusion = (f32[128,128]{1,0:T(8,128)S(1)}, f32[128,128]{1,0:T(8,128)S(1)}, f32[128,128]{1,0:T(8,128)S(1)}, f32[128,128]{1,0:T(8,128)S(1)}, f32[1...) fusion(f32[128,128]{1,0:T(8,128)S(1)} %copy.215, ...), kind=kLoop, calls=%fused_computation.4 | loop fusion | flops 83755008 | bytes 1654784
  100.8 15.5 %all-to-all-start = ((f32[32,4,128]{2,1,0:T(4,128)}), f32[32,4,128]{2,1,0:T(4,128)S(1)}, u32[]{:S(2)}, u32[]{:S(2)}) async-start(f32[32,4,128]{2,1,0:T(4,128)} %broadcast_in_dim.152), calls=%async_computation | async-start | bytes 131072 | tf_op jit(solution)/shard_map/all_to_all | solution.py:26
  116.3 13.1 %all-to-all-done = f32[32,4,128]{2,1,0:T(4,128)S(1)} async-done(((f32[32,4,128]{2,1,0:T(4,128)}), f32[32,4,128]{2,1,0:T(4,128)S(1)}, u32[]{:S(2)}, u32[]{:S(2)}) %all-to-all-start) | async-done | bytes 65568 | tf_op jit(solution)/shard_map/all_to_all | solution.py:26
  131.1 1.6 gather_fusion.1
  132.7 7.0 %all-to-all-start.2 = ((f32[16,8,1,1024]{3,1,2,0:T(8,128)}), f32[16,8,1,1024]{3,1,2,0:T(8,128)S(1)}, u32[]{:S(2)}, u32[]{:S(2)}) async-start(f32[16,8,1,1024]{3,1,2,0:T(8,128)} %bitcast.70), calls=%async_computation.2 | async-start | bytes 1048576 | tf_op jit(solution)/shard_map/all_to_all | solution.py:214
  139.8 28.5 %all-reduce = (f32[128]{0:T(128)S(1)}, f32[128]{0:T(128)S(1)}, f32[128]{0:T(128)S(1)}) all-reduce(f32[128]{0:T(128)S(1)} %convolution_bitcast_fusion.4, f32[128]{0:T(128)S(1)} %convolution_bitcast_fusion.3, f32[128]{0:T(128)S(1)} %convolution_bitcast_fusion.1), channel_id=1, replica_groups=mesh['tm_0'=16,'tm_1'=2,'batch_0'=4,'batch_1'=4] {'tm_0'}, use_global_device_ids=true, to_apply=%region_9.10 | all-reduce | flops 384 | bytes 3072 | tf_op jit(solution)/shard_map/psum | solution.py:72
  168.2 2.5 %all-reduce.3 = (f32[128]{0:T(128)S(1)}, f32[128]{0:T(128)S(1)}, f32[128]{0:T(128)S(1)}) all-reduce(f32[128]{0:T(128)S(1)} %get-tuple-element.40, f32[128]{0:T(128)S(1)} %get-tuple-element.41, f32[128]{0:T(128)S(1)} %get-tuple-element.42), channel_id=1, replica_groups=mesh['tm_0'=16,'tm_1'=2,'batch_0'=4,'batch_1'=4] {'tm_1'}, use_global_device_ids=true, to_apply=%region_10.11 | all-reduce | flops 384 | bytes 3072 | tf_op jit(solution)/shard_map/psum | solution.py:72
  170.7 10.8 %all-reduce.2 = (f32[128]{0:T(128)S(1)}, f32[128]{0:T(128)S(1)}, f32[128]{0:T(128)S(1)}) all-reduce(f32[128]{0:T(128)S(1)} %get-tuple-element.49, f32[128]{0:T(128)S(1)} %get-tuple-element.50, f32[128]{0:T(128)S(1)} %get-tuple-element.51), channel_id=1, replica_groups=mesh['tm_0'=16,'tm_1'=2,'batch_0'=4,'batch_1'=4] {'batch_0'}, use_global_device_ids=true, to_apply=%region_11.12 | all-reduce | flops 384 | bytes 3072 | tf_op jit(solution)/shard_map/psum | solution.py:72
  181.5 10.4 %all-reduce.1 = (f32[128]{0:T(128)S(1)}, f32[128]{0:T(128)S(1)}, f32[128]{0:T(128)S(1)}) all-reduce(f32[128]{0:T(128)S(1)} %get-tuple-element.46, f32[128]{0:T(128)S(1)} %get-tuple-element.47, f32[128]{0:T(128)S(1)} %get-tuple-element.48), channel_id=1, replica_groups=mesh['tm_0'=16,'tm_1'=2,'batch_0'=4,'batch_1'=4] {'batch_1'}, use_global_device_ids=true, to_apply=%region_12.13 | all-reduce | flops 384 | bytes 3072 | tf_op jit(solution)/shard_map/psum | solution.py:72
  192.9 1.6 gather_fusion
  194.5 3.6 %all-to-all-start.1 = ((f32[16,8,1,1024]{3,1,2,0:T(8,128)}), f32[16,8,1,1024]{3,1,2,0:T(8,128)S(1)}, u32[]{:S(2)}, u32[]{:S(2)}) async-start(f32[16,8,1,1024]{3,1,2,0:T(8,128)} %bitcast.62), calls=%async_computation.1 | async-start | bytes 1048576 | tf_op jit(solution)/shard_map/all_to_all | solution.py:213
  199.0 1.1 copy.123
  200.1 8.0 %all-to-all-done.1 = f32[16,8,1,1024]{3,1,2,0:T(8,128)S(1)} async-done(((f32[16,8,1,1024]{3,1,2,0:T(8,128)}), f32[16,8,1,1024]{3,1,2,0:T(8,128)S(1)}, u32[]{:S(2)}, u32[]{:S(2)}) %all-to-all-start.1) | async-done | bytes 524320 | tf_op jit(solution)/shard_map/all_to_all | solution.py:213
  208.1 1.1 copy.119
  (245 shorter events, 18.0 us)
Async XLA Ops:
  0.6 3.2 %copy-start.18 = (s32[128]{0:T(128)S(1)}, s32[128]{0:T(128)}, u32[]{:S(2)}) copy-start(s32[128]{0:T(128)} %param.8) | copy-start | bytes 1540
  0.6 3.3 %copy-start.19 = (s32[128]{0:T(128)S(1)}, s32[128]{0:T(128)}, u32[]{:S(2)}) copy-start(s32[128]{0:T(128)} %param.9) | copy-start | bytes 1540
  1.9 5.9 %collective-permute-start = (f32[128,1]{0,1:T(1,128)S(1)}, f32[128,1]{0,1:T(1,128)S(1)}, u32[]{:S(2)}, u32[]{:S(2)}) collective-permute-start(f32[128,1]{0,1:T(1,128)S(1)} %slice.444), channel_id=1, source_target_pairs={{16,0},{32,16},{48,32},{64,48},{80,64},{96,80},{112,96},{128,112},... | collective-permute-start | bytes 1544 | tf_op jit(solution)/shard_map/ppermute | solution.py:21
  5.5 1.0 copy-start.1
  6.5 1.0 copy-start.2
  8.1 1.7 copy-start
  10.1 40.6 %copy-start.16 = (pred[128,128]{0,1:T(8,128)(4,1)}, pred[128,128]{0,1:T(8,128)(4,1)S(1)}, u32[]{:S(2)}) copy-start(pred[128,128]{0,1:T(8,128)(4,1)S(1)} %get-tuple-element.70) | copy-start | bytes 49156
  11.4 41.0 %copy-start.14 = (pred[128,128]{0,1:T(8,128)(4,1)}, pred[128,128]{0,1:T(8,128)(4,1)S(1)}, u32[]{:S(2)}) copy-start(pred[128,128]{0,1:T(8,128)(4,1)S(1)} %get-tuple-element.68) | copy-start | bytes 49156
  13.8 38.9 %copy-start.6 = (pred[128,128]{0,1:T(8,128)(4,1)}, pred[128,128]{0,1:T(8,128)(4,1)S(1)}, u32[]{:S(2)}) copy-start(pred[128,128]{0,1:T(8,128)(4,1)S(1)} %get-tuple-element.64) | copy-start | bytes 49156
  15.0 37.8 %copy-start.8 = (pred[128,128]{0,1:T(8,128)(4,1)}, pred[128,128]{0,1:T(8,128)(4,1)S(1)}, u32[]{:S(2)}) copy-start(pred[128,128]{0,1:T(8,128)(4,1)S(1)} %get-tuple-element.62) | copy-start | bytes 49156
  16.2 36.7 %copy-start.10 = (pred[128,128]{0,1:T(8,128)(4,1)}, pred[128,128]{0,1:T(8,128)(4,1)S(1)}, u32[]{:S(2)}) copy-start(pred[128,128]{0,1:T(8,128)(4,1)S(1)} %get-tuple-element.60) | copy-start | bytes 49156
  17.5 35.7 %copy-start.12 = (pred[128,128]{0,1:T(8,128)(4,1)}, pred[128,128]{0,1:T(8,128)(4,1)S(1)}, u32[]{:S(2)}) copy-start(pred[128,128]{0,1:T(8,128)(4,1)S(1)} %get-tuple-element.58) | copy-start | bytes 49156
  53.2 0.6 copy-start.3
  96.8 0.8 copy-start.5
  97.1 0.9 copy-start.4
  97.8 0.7 copy-start.13
  97.8 0.8 copy-start.11
  98.0 0.7 copy-start.9
  98.0 0.9 copy-start.7
  98.0 1.1 copy-start.15
  98.0 1.2 copy-start.17
  100.8 28.6 %all-to-all-start = ((f32[32,4,128]{2,1,0:T(4,128)}), f32[32,4,128]{2,1,0:T(4,128)S(1)}, u32[]{:S(2)}, u32[]{:S(2)}) async-start(f32[32,4,128]{2,1,0:T(4,128)} %broadcast_in_dim.152), calls=%async_computation | async-start | bytes 131072 | tf_op jit(solution)/shard_map/all_to_all | solution.py:26
  132.7 61.7 %all-to-all-start.2 = ((f32[16,8,1,1024]{3,1,2,0:T(8,128)}), f32[16,8,1,1024]{3,1,2,0:T(8,128)S(1)}, u32[]{:S(2)}, u32[]{:S(2)}) async-start(f32[16,8,1,1024]{3,1,2,0:T(8,128)} %bitcast.70), calls=%async_computation.2 | async-start | bytes 1048576 | tf_op jit(solution)/shard_map/all_to_all | solution.py:214
  194.5 13.6 %all-to-all-start.1 = ((f32[16,8,1,1024]{3,1,2,0:T(8,128)}), f32[16,8,1,1024]{3,1,2,0:T(8,128)S(1)}, u32[]{:S(2)}, u32[]{:S(2)}) async-start(f32[16,8,1,1024]{3,1,2,0:T(8,128)} %bitcast.62), calls=%async_computation.1 | async-start | bytes 1048576 | tf_op jit(solution)/shard_map/all_to_all | solution.py:213
where the time goes:
time: 210 us; the launch traced here: 209 us
  other arithmetic  78.5 us (37%)
  blocking collectives  52.1 us (25%)
  starting transfers between devices  28 us (13%)
  waiting for transfers between devices  21.1 us (10%)
  local copies, waits for them, and re-layouts  18.3 us (9%)
  matrix products  9 us (4%)
  between operations  2.21 us (1%)
    unnamed x15, other arithmetic  75.6 us
    psum x4, blocking collectives, over_axes(): value = lax.psum(value, axis)  52.1 us
    all_to_all x1, starting transfers between devices, copy_for_each(): lax.all_to_all(jnp.broadcast_to(value[None], (size, *value.shape)), axis,...  15.5 us
    all_to_all x1, waiting for transfers between devices, copy_for_each(): lax.all_to_all(jnp.broadcast_to(value[None], (size, *value.shape)), axis,...  13.1 us
    all_to_all x1, waiting for transfers between devices, on_device(): lax.all_to_all(norm_buffer, BATCH, split_axis=0, concat_axis=2, tiled=True)  7.96 us
    dot_general x8, matrix products, block_chain(): before = jnp.dot(breaks, lower, precision=lax.Precision.HIGHEST)  7.93 us
    unnamed x72, local copies, waits for them, and re-layouts  7.27 us
    all_to_all x1, starting transfers between devices, on_device(): lax.all_to_all(ret_buffer, BATCH, split_axis=0, concat_axis=2, tiled=True)  7.03 us
  transfers between devices with their start and end apart: 4, of which 2 were waited for; matrix products, arithmetic and copies ran while one was open for 3% of the time, Pallas kernels for 0%

commit v1 on v0

v1 whole, which is shorter than its diff:
```python
import jax
import jax.numpy as jnp
from jax import lax
from jax.experimental import pallas as pl
from jax.experimental.pallas import tpu as pltpu
from jax.sharding import PartitionSpec as P

MESH = pl.DeviceIdType.MESH
F32 = jnp.float32
BF16 = jnp.bfloat16
GAMMA_RATE = 0.9995
ALPHA_RATE = 0.05
EPSILON = 1e-06
LANES = 128
TILE = 8
GROUP_ROWS = 16


def second_rate(lengths):
    return GAMMA_RATE * (1.0 - 1.0 / (ALPHA_RATE * lengths))


def squarings(rate, count):
    powers = [rate]
    for _ in range(count):
        powers.append(powers[-1] * powers[-1])
    return powers


def lane_powers(powers, exponent):
    result = None
    for bit, power in enumerate(powers):
        factor = jnp.where((exponent & (1 << bit)) != 0, power, 1.0)
        result = factor if result is None else result * factor
    return result


def split(value, terms):
    pieces = []
    for _ in range(terms):
        piece = value.astype(BF16)
        pieces.append(piece)
        value = value - piece.astype(F32)
    return pieces


def fused(
    n_tm,
    n_batch,
    len_ref,
    grp_ref,
    rew_hbm,
    val_hbm,
    end_hbm,
    adv_out,
    gadv_out,
    gret_out,
    rew,
    val,
    end,
    loc_r,
    loc_a,
    tail_a,
    len_cols,
    summary,
    send_bulk,
    recv_bulk,
    send_z,
    recv_z,
    send_stat,
    recv_stat,
    done_r,
    done_a,
    in_sem,
    out_sem,
    bulk_ss,
    bulk_rs,
    z_ss,
    z_rs,
    stat_ss,
    stat_rs,
    ready_sem,
):
    height, span = rew.shape
    count = span // LANES
    chunks = 4
    chunk_rows = height // chunks
    tm = lax.axis_index("tm")
    me = lax.axis_index("batch")
    core = lax.rem(tm, 2)
    partner = tm + 1 - 2 * core
    start = tm * span

    def loads(k):
        rows = pl.ds(k * chunk_rows, chunk_rows)
        return [
            pltpu.make_async_copy(source.at[rows, :], target.at[rows, :], in_sem.at[k, n])
            for n, (source, target) in enumerate(((rew_hbm, rew), (val_hbm, val), (end_hbm, end)))
        ]

    for k in range(chunks):
        for copy in loads(k):
            copy.start()

    barrier = pltpu.get_barrier_semaphore()
    for d in range(1, n_batch):
        pl.semaphore_signal(
            barrier,
            inc=1,
            device_id={"tm": tm - core, "batch": lax.rem(me + d, n_batch)},
            device_id_type=MESH,
        )
    for d in range(1, n_tm // 2):
        pl.semaphore_signal(
            barrier,
            inc=1,
            device_id={"tm": lax.rem(tm - core + 2 * d, n_tm) + 1, "batch": me},
            device_id_type=MESH,
        )
    pl.semaphore_signal(
        barrier, inc=1, device_id={"tm": partner, "batch": me}, device_id_type=MESH
    )

    lane_row = lax.broadcasted_iota(jnp.int32, (1, LANES), 1)
    lengths_row = len_ref[...]
    len_cols[...] = jnp.broadcast_to(lengths_row, (height, LANES)).T

    lane = lax.broadcasted_iota(jnp.int32, (GROUP_ROWS, LANES), 1)
    lane_f = lane.astype(F32)
    gamma_powers = [GAMMA_RATE ** (1 << bit) for bit in range(8)]
    up_r = lane_powers(gamma_powers[:7], lane)
    down_r = 1.0 / up_r
    to_end_r = down_r * gamma_powers[7]

    def scan_rows(g, _):
        rows = pl.ds(pl.multiple_of(g * GROUP_ROWS, GROUP_ROWS), GROUP_ROWS)
        lengths = len_cols[rows, :]
        rate = second_rate(lengths.astype(F32))
        powers = squarings(rate, 7)
        up_a = lane_powers(powers[:7], lane)
        down_a = 1.0 / up_a
        to_end_a = down_a * powers[7]
        limit = lengths - start
        rolled_next = None
        state = []
        last_break = None
        for j in reversed(range(count)):
            cols = pl.ds(j * LANES, LANES)
            place = lane + j * LANES
            reward, value, ends = rew[rows, cols], val[rows, cols], end[rows, cols]
            inside = place < limit
            carry_on = (place < limit - 1) & (ends != 1)
            rolled = pltpu.roll(value, LANES - 1, 1)
            after = 0.0 if rolled_next is None else rolled_next
            value_next = jnp.where(lane == LANES - 1, after, rolled)
            rolled_next = rolled
            reward_in = jnp.where(inside, reward, 0.0)
            follow = jnp.where(carry_on, value_next, 0.0)
            delta = jnp.where(inside, reward_in + GAMMA_RATE * follow - value, 0.0)
            stop = jnp.where(carry_on, float(LANES), lane_f)
            here = jnp.where(carry_on, -1.0, lane_f + float(j * LANES))
            last_break = here if last_break is None else jnp.maximum(last_break, here)
            for bit in range(7):
                step = 1 << bit
                moved = pltpu.roll(stop, LANES - step, 1)
                stop = jnp.minimum(stop, jnp.where(lane < LANES - step, moved, float(LANES)))
            reach = jnp.minimum(stop, float(LANES - 1)) - lane_f
            open_end = stop == float(LANES)
            sum_r, sum_a = reward_in * up_r, delta * up_a
            for bit in range(7):
                step = 1 << bit
                linked = reach >= float(step)
                sum_r = sum_r + jnp.where(linked, pltpu.roll(sum_r, LANES - step, 1), 0.0)
                sum_a = sum_a + jnp.where(linked, pltpu.roll(sum_a, LANES - step, 1), 0.0)
            state.append((j, sum_r * down_r, sum_a * down_a, open_end))
        final_break = jnp.max(last_break, axis=1, keepdims=True)
        carry_r = carry_a = None
        scale = to_end_a
        totals = None
        for j, part_r, part_a, open_end in state:
            cols = pl.ds(j * LANES, LANES)
            if carry_r is not None:
                part_r = part_r + jnp.where(open_end, to_end_r, 0.0) * carry_r
                part_a = part_a + jnp.where(open_end, to_end_a, 0.0) * carry_a
                scale = scale * powers[7]
            carry_r = jnp.broadcast_to(part_r[:, :1], part_r.shape)
            carry_a = jnp.broadcast_to(part_a[:, :1], part_a.shape)
            tail = jnp.where(lane_f + float(j * LANES) > final_break, scale, 0.0)
            loc_r[rows, cols] = part_r
            loc_a[rows, cols] = part_a
            tail_a[rows, cols] = tail
            terms = (part_a, part_a * part_a, part_a * tail, tail, tail * tail)
            totals = terms if totals is None else [s + t for s, t in zip(totals, terms)]
        first_value = jnp.broadcast_to(val[rows, pl.ds(0, LANES)][:, :1], carry_a.shape)
        columns = [carry_r, carry_a + first_value * (GAMMA_RATE / rate), float(span - 1) - final_break]
        columns += [jnp.sum(total, axis=1, keepdims=True) for total in totals]
        line = jnp.zeros((GROUP_ROWS, LANES), F32)
        for n, column in enumerate(columns):
            line = jnp.where(lane == n, column, line)
        summary[rows, :] = line
        return 0

    per_chunk = chunk_rows // GROUP_ROWS
    for k in range(chunks):
        for copy in loads(k):
            copy.wait()
        lax.fori_loop(k * per_chunk, (k + 1) * per_chunk, scan_rows, 0)

    send_z[...] = summary[...].T[:TILE]
    recv_z[tm] = send_z[...]

    order = lax.broadcasted_iota(jnp.int32, (height, height), 0) == jnp.broadcast_to(
        grp_ref[...], (height, height)
    )
    order = jnp.where(order, 1.0, 0.0).astype(BF16)
    twice = jnp.concatenate([order, order], axis=1)
    thrice = jnp.concatenate([order, order, order], axis=1)
    wide = 2 * LANES

    def permute(c, _):
        cols = pl.ds(pl.multiple_of(c * wide, wide), wide)
        for n, source in enumerate((loc_r, loc_a)):
            pieces = jnp.concatenate(split(source[:, cols], 2), axis=0)
            moved = jnp.dot(twice, pieces, preferred_element_type=F32)
            send_bulk[:, n * TILE : (n + 1) * TILE, cols] = moved.reshape(n_batch, TILE, wide)
        return 0

    lax.fori_loop(0, span // wide, permute, 0)

    @pl.when(core == 0)
    def _():
        pl.semaphore_wait(barrier, 2 * n_batch - 1)
        pl.semaphore_signal(
            ready_sem, inc=1, device_id={"tm": partner, "batch": me}, device_id_type=MESH
        )

    @pl.when(core == 1)
    def _():
        pl.semaphore_wait(ready_sem, 1)

    def bulk(to, slot):
        return pltpu.make_async_remote_copy(
            src_ref=send_bulk.at[to],
            dst_ref=recv_bulk.at[slot],
            send_sem=bulk_ss.at[to],
            recv_sem=bulk_rs.at[slot],
            device_id={"tm": tm, "batch": to},
            device_id_type=MESH,
        )

    def send_one(d, _):
        bulk(lax.rem(me + d, n_batch), me).start()
        return 0

    lax.fori_loop(1, n_batch, send_one, 0)

    @pl.when(core == 1)
    def _():
        pl.semaphore_wait(barrier, n_tm - 1)
        pl.semaphore_signal(
            ready_sem, inc=1, device_id={"tm": partner, "batch": me}, device_id_type=MESH
        )

    @pl.when(core == 0)
    def _():
        pl.semaphore_wait(ready_sem, 1)

    def along(to, slot):
        return pltpu.make_async_remote_copy(
            src_ref=send_z,
            dst_ref=recv_z.at[slot],
            send_sem=z_ss.at[to],
            recv_sem=z_rs.at[slot],
            device_id={"tm": to, "batch": me},
            device_id_type=MESH,
        )

    def tell_one(d, _):
        along(lax.rem(tm + d, n_tm), tm).start()
        return 0

    lax.fori_loop(1, n_tm, tell_one, 0)
    recv_bulk[me] = send_bulk[me]

    def hear_one(d, _):
        along(lax.rem(tm + d, n_tm), lax.rem(tm + d, n_tm)).wait_recv()
        return 0

    lax.fori_loop(1, n_tm, hear_one, 0)

    lengths_f = lengths_row.astype(F32)
    whole_a = squarings(second_rate(lengths_f), 10)[10]
    whole_r = GAMMA_RATE**span
    whole_a = jnp.broadcast_to(whole_a, (TILE, LANES))
    zero = whole_a * 0.0

    def chain(k, carried):
        block = n_tm - 1 - k
        into_r, into_a, own_r, own_a, first, second = carried
        tile = recv_z[block]
        piece = [jnp.broadcast_to(tile[n : n + 1], (TILE, LANES)) for n in range(TILE)]
        mine = jnp.where(block == tm, 1.0, 0.0)
        own_r = own_r + mine * into_r
        own_a = own_a + mine * into_a
        first = first + piece[3] + piece[6] * into_a
        second = second + piece[4] + into_a * (2.0 * piece[5] + piece[7] * into_a)
        whole = piece[2] == float(span)
        into_r = piece[0] + jnp.where(whole, whole_r, 0.0) * into_r
        into_a = piece[1] + jnp.where(whole, whole_a, 0.0) * into_a
        return into_r, into_a, own_r, own_a, first, second

    _, _, own_r, own_a, first, second = lax.fori_loop(0, n_tm, chain, (zero,) * 6)
    lines = jnp.concatenate(
        [line[:1] for line in (own_r, own_a, first, second, send_z[2:3], lengths_f)]
        + [jnp.zeros((height - 6, LANES), F32)],
        axis=0,
    )
    send_stat[...] = lax.dot_general(
        thrice,
        jnp.concatenate(split(lines, 3), axis=1),
        (((1,), (1,)), ((), ())),
        preferred_element_type=F32,
    )
    recv_stat[me] = send_stat[pl.ds(pl.multiple_of(me * TILE, TILE), TILE), :]

    def stat(to, slot):
        return pltpu.make_async_remote_copy(
            src_ref=send_stat.at[pl.ds(pl.multiple_of(to * TILE, TILE), TILE), :],
            dst_ref=recv_stat.at[slot],
            send_sem=stat_ss.at[to],
            recv_sem=stat_rs.at[slot],
            device_id={"tm": tm, "batch": to},
            device_id_type=MESH,
        )

    def send_stats(d, _):
        stat(lax.rem(me + d, n_batch), me).start()
        return 0

    lax.fori_loop(1, n_batch, send_stats, 0)

    summary[...] = lines.T

    def own_rows(g, _):
        rows = pl.ds(pl.multiple_of(g * GROUP_ROWS, GROUP_ROWS), GROUP_ROWS)
        into = jnp.broadcast_to(summary[rows, :][:, 1:2], (GROUP_ROWS, LANES))
        for j in range(count):
            cols = pl.ds(j * LANES, LANES)
            end_values = loc_a[rows, cols] + tail_a[rows, cols] * into
            loc_a[rows, cols] = end_values
        return 0

    lax.fori_loop(0, height // GROUP_ROWS, own_rows, 0)
    own_copy = pltpu.make_async_copy(loc_a, adv_out, out_sem.at[0])
    own_copy.start()

    def hear_stats(d, _):
        slot = lax.rem(me + d, n_batch)
        stat(slot, slot).wait_recv()
        return 0

    lax.fori_loop(1, n_batch, hear_stats, 0)
    total = recv_stat[0]
    for i in range(1, n_batch):
        total = total + recv_stat[i]
    counted = total[:, 5:6]
    mean = total[:, 2:3] / counted
    var = total[:, 3:4] / counted - mean * mean
    mean = jnp.broadcast_to(mean, (TILE, LANES))
    inverse = jnp.broadcast_to(1.0 / jnp.sqrt(var + EPSILON), (TILE, LANES))

    def finish(d, _):
        i = lax.rem(me + d, n_batch)

        @pl.when(d > 0)
        def _():
            bulk(i, i).wait_recv()

        facts = recv_stat[i]
        into_r = jnp.broadcast_to(facts[:, 0:1], (TILE, LANES))
        into_a = jnp.broadcast_to(facts[:, 1:2], (TILE, LANES))
        last = float(span - 1) - jnp.broadcast_to(facts[:, 4:5], (TILE, LANES))
        lengths = jnp.broadcast_to(facts[:, 5:6], (TILE, LANES))
        powers = squarings(second_rate(lengths), 7)
        scale_a = powers[7] / lane_powers(powers[:7], lane[:TILE])
        scale_r = to_end_r[:TILE]
        limit = lengths - start.astype(F32)
        rows = pl.ds(i, TILE, stride=n_batch)
        for j in reversed(range(count)):
            cols = pl.ds(j * LANES, LANES)
            place = lane_f[:TILE] + float(j * LANES)
            carried = place > last
            ret = recv_bulk[i, :TILE, cols] + jnp.where(carried, scale_r, 0.0) * into_r
            adv = recv_bulk[i, TILE:, cols] + jnp.where(carried, scale_a, 0.0) * into_a
            done_r[j, rows, :] = ret
            done_a[j, rows, :] = jnp.where(place < limit, (adv - mean) * inverse, 0.0)
            scale_r = scale_r * gamma_powers[7]
            scale_a = scale_a * powers[7]
        return 0

    lax.fori_loop(0, n_batch, finish, 0)

    def stores(j):
        cols = pl.ds(j * LANES, LANES)
        return [
            pltpu.make_async_copy(source.at[j], target.at[:, cols], out_sem.at[1 + 2 * j + n])
            for n, (source, target) in enumerate(((done_r, gret_out), (done_a, gadv_out)))
        ]

    for j in range(count):
        for copy in stores(j):
            copy.start()

    def sent(d, _):
        to = lax.rem(me + d, n_batch)
        bulk(to, me).wait_send()
        stat(to, me).wait_send()
        return 0

    lax.fori_loop(1, n_batch, sent, 0)

    def told(d, _):
        along(lax.rem(tm + d, n_tm), tm).wait_send()
        return 0

    lax.fori_loop(1, n_tm, told, 0)
    own_copy.wait()
    for j in range(count):
        for copy in stores(j):
            copy.wait()


def solution(mesh):
    n_tm, n_batch = mesh.shape["tm"], mesh.shape["batch"]

    def on_device(rewards, values, episode_ends, lengths, groups):
        height, span = rewards.shape
        block = pltpu.VMEM((height, span), F32)
        square = pltpu.VMEM((height, LANES), F32)
        out = jax.ShapeDtypeStruct((height, span), F32)

        def kernel(*refs):
            fused(n_tm, n_batch, *refs)

        return pl.pallas_call(
            kernel,
            out_shape=(out, out, out),
            in_specs=[pl.BlockSpec(memory_space=pltpu.VMEM)] * 2
            + [pl.BlockSpec(memory_space=pl.ANY)] * 3,
            out_specs=[pl.BlockSpec(memory_space=pl.ANY)] * 3,
            scratch_shapes=[
                block,
                block,
                pltpu.VMEM((height, span), jnp.int32),
                block,
                block,
                block,
                pltpu.VMEM((height, LANES), jnp.int32),
                square,
                pltpu.VMEM((n_batch, 2 * TILE, span), F32),
                pltpu.VMEM((n_batch, 2 * TILE, span), F32),
                pltpu.VMEM((TILE, LANES), F32),
                pltpu.VMEM((n_tm, TILE, LANES), F32),
                square,
                pltpu.VMEM((n_batch, TILE, LANES), F32),
                pltpu.VMEM((span // LANES, height, LANES), F32),
                pltpu.VMEM((span // LANES, height, LANES), F32),
                pltpu.SemaphoreType.DMA((4, 3)),
                pltpu.SemaphoreType.DMA((1 + 2 * (span // LANES),)),
                pltpu.SemaphoreType.DMA((n_batch,)),
                pltpu.SemaphoreType.DMA((n_batch,)),
                pltpu.SemaphoreType.DMA((n_tm,)),
                pltpu.SemaphoreType.DMA((n_tm,)),
                pltpu.SemaphoreType.DMA((n_batch,)),
                pltpu.SemaphoreType.DMA((n_batch,)),
                pltpu.SemaphoreType.REGULAR,
            ],
            compiler_params=pltpu.CompilerParams(collective_id=0, has_side_effects=True),
        )(lengths.reshape(1, height), groups.reshape(1, height), rewards, values, episode_ends)

    return jax.shard_map(
        on_device,
        mesh=mesh,
        in_specs=(
            P("batch", "tm"),
            P("batch", "tm"),
            P("batch", "tm"),
            P("batch"),
            P("batch"),
        ),
        out_specs=(P("batch", "tm"), P("batch", "tm"), P("batch", "tm")),
        check_vma=False,
    )
```

time: 210 us -> 54.1 us (0.26)
  the two profiles are of different devices: /device:TPU:32 before, /device:TPU:1 now
where the time goes in v1:
time: 54.1 us; the launch traced here: 53.9 us
  Pallas kernels  49.2 us (91%)
  local copies, waits for them, and re-layouts  3.97 us (7%)
  between operations  0.65 us (1%)
    pallas_call x1, Pallas kernels, on_device(): pl.pallas_call(kernel, out_shape=(out, out, out), in_specs=[pl.BlockSpec(...  49.2 us
    unnamed x7, local copies, waits for them, and re-layouts  3.97 us

profile of v1, /device:TPU:1, one launch (start us, length us, event | category | flops | bytes accessed | tf_op | source)
XLA Modules:
  0.0 53.9 jit_solution(8075563078137223150)
XLA Ops:
  0.6 49.2 %shard_map.76 = (f32[128,1024]{1,0:T(8,128)}, f32[128,1024]{1,0:T(8,128)}, f32[128,1024]{1,0:T(8,128)}) custom-call(s32[1,128]{1,0:T(1,128)} %bitcast.2, s32[1,128]{1,0:T(1,128)} %bitcast.3, f32[128,1024]{1,0:T(8,128)} %refs_2_.1, f32[128,1024]{1,0:T(8,128)} %refs_3_.1, s32[128,1024]{1,0:T(8,128)} %refs_4_.1), custom_call_target="tpu_custom_call" | custom-call | tf_op jit(solution)/shard_map/pallas_call | solution.py:445
  49.9 0.0 copy-start.1
  49.9 1.9 %copy.11 = f32[128,1024]{1,0:T(8,128)} copy(f32[128,1024]{1,0:T(8,128)} %get-tuple-element.6) | data formatting | bytes 1048576
  51.8 0.0 copy-done.1
  51.8 0.0 copy-start
  51.8 0.8 %copy.12 = f32[128,1024]{1,0:T(8,128)} copy(f32[128,1024]{1,0:T(8,128)S(1)} %copy-done.1) | data formatting | bytes 1048576
  52.6 0.4 copy-done
  53.1 0.8 %copy.13 = f32[128,1024]{1,0:T(8,128)} copy(f32[128,1024]{1,0:T(8,128)S(1)} %copy-done) | data formatting | bytes 1048576
Async XLA Ops:
  49.9 2.0 %copy-start.1 = (f32[128,1024]{1,0:T(8,128)S(1)}, f32[128,1024]{1,0:T(8,128)}, u32[]{:S(2)}) copy-start(f32[128,1024]{1,0:T(8,128)} %get-tuple-element.7) | copy-start | bytes 1572868
  51.8 1.2 %copy-start = (f32[128,1024]{1,0:T(8,128)S(1)}, f32[128,1024]{1,0:T(8,128)}, u32[]{:S(2)}) copy-start(f32[128,1024]{1,0:T(8,128)} %get-tuple-element.8) | copy-start | bytes 1572868

commit v2 on v1

v2 whole, which is shorter than its diff:
```python
import jax
import jax.numpy as jnp
from jax import lax
from jax.experimental import pallas as pl
from jax.experimental.pallas import tpu as pltpu
from jax.sharding import PartitionSpec as P

MESH = pl.DeviceIdType.MESH
F32 = jnp.float32
BF16 = jnp.bfloat16
GAMMA_RATE = 0.9995
ALPHA_RATE = 0.05
EPSILON = 1e-06
LANES = 128
TILE = 8
STRIDE = 136


def second_rate(lengths):
    return GAMMA_RATE * (1.0 - 1.0 / (ALPHA_RATE * lengths))


def squarings(rate, count):
    powers = [rate]
    for _ in range(count):
        powers.append(powers[-1] * powers[-1])
    return powers


def lane_powers(powers, exponent):
    result = None
    for bit, power in enumerate(powers):
        factor = jnp.where((exponent & (1 << bit)) != 0, power, 1.0)
        result = factor if result is None else result * factor
    return result


def split(value, terms):
    pieces = []
    for _ in range(terms):
        piece = value.astype(BF16)
        pieces.append(piece)
        value = value - piece.astype(F32)
    return pieces


def fused(
    n_tm,
    n_batch,
    len_ref,
    grp_ref,
    rew_hbm,
    val_hbm,
    end_hbm,
    own_out,
    recv_bulk,
    recv_stat,
    rew,
    val,
    end,
    time_rew,
    time_val,
    time_end,
    time_r,
    time_a,
    time_m,
    send_bulk,
    send_z,
    recv_z,
    send_stat,
    in_sem,
    bulk_ss,
    bulk_rs,
    z_ss,
    z_rs,
    stat_ss,
    stat_rs,
    ready_sem,
):
    height, span = rew.shape
    count = span // LANES
    chunks = 4
    chunk_cols = span // chunks
    tm = lax.axis_index("tm")
    me = lax.axis_index("batch")
    core = lax.rem(tm, 2)
    partner = tm + 1 - 2 * core
    start = tm * span

    def loads(k):
        cols = pl.ds(k * chunk_cols, chunk_cols)
        return [
            pltpu.make_async_copy(source.at[:, cols], target.at[:, cols], in_sem.at[k, n])
            for n, (source, target) in enumerate(((rew_hbm, rew), (val_hbm, val), (end_hbm, end)))
        ]

    for k in range(chunks):
        for copy in loads(k):
            copy.start()

    barrier = pltpu.get_barrier_semaphore()
    for d in range(1, n_batch):
        pl.semaphore_signal(
            barrier,
            inc=1,
            device_id={"tm": tm - core, "batch": lax.rem(me + d, n_batch)},
            device_id_type=MESH,
        )
    for d in range(1, n_tm // 2):
        pl.semaphore_signal(
            barrier,
            inc=1,
            device_id={"tm": lax.rem(tm - core + 2 * d, n_tm) + 1, "batch": me},
            device_id_type=MESH,
        )
    pl.semaphore_signal(
        barrier, inc=1, device_id={"tm": partner, "batch": me}, device_id_type=MESH
    )

    lengths_row = len_ref[...]

    for k in range(chunks):
        for copy in loads(k):
            copy.wait()
        for j in range(k * (count // chunks), (k + 1) * (count // chunks)):
            rows = pl.ds(j * STRIDE, LANES)
            for source, target in ((rew, time_rew), (val, time_val), (end, time_end)):
                target[rows, :] = source[:, j * LANES : (j + 1) * LANES].T

    sublane = lax.broadcasted_iota(jnp.int32, (TILE, LANES), 0)
    lengths = jnp.broadcast_to(lengths_row, (TILE, LANES))
    limit = lengths - (start + sublane * LANES)
    rate = second_rate(lengths.astype(F32))
    whole_seg_a = squarings(rate, 7)[7]
    whole_seg_r = GAMMA_RATE**LANES

    def terms(k, value_next):
        at = pl.ds(k, TILE, stride=STRIDE)
        reward, value, ends = time_rew[at, :], time_val[at, :], time_end[at, :]
        inside = k < limit
        carry_on = (k < limit - 1) & (ends != 1)
        reward_in = jnp.where(inside, reward, 0.0)
        follow = jnp.where(carry_on, GAMMA_RATE * value_next, 0.0)
        delta = jnp.where(inside, reward_in + follow - value, 0.0)
        return at, value, carry_on, reward_in, delta

    def heads(step, carried):
        value_next, sum_r, sum_a, whole = carried
        _, value, carry_on, reward_in, delta = terms(LANES - 1 - step, value_next)
        sum_r = reward_in + jnp.where(carry_on, GAMMA_RATE * sum_r, 0.0)
        sum_a = delta + jnp.where(carry_on, rate * sum_a, 0.0)
        return value, sum_r, sum_a, jnp.where(carry_on, whole, 0.0)

    nought = limit.astype(F32) * 0.0
    first_value, head_r, head_a, whole = lax.fori_loop(
        0, LANES, heads, (nought, nought, nought, nought + 1.0), unroll=8
    )
    head_a = head_a + first_value * (GAMMA_RATE / rate)
    into_r = into_a = nought
    into_m = jnp.where(sublane == TILE - 1, 1.0, nought)
    for _ in range(TILE - 1):
        into_r = head_r + whole * whole_seg_r * into_r
        into_a = head_a + whole * whole_seg_a * into_a
        into_m = whole * whole_seg_a * into_m
        last = sublane == TILE - 1
        into_r = jnp.where(last, 0.0, pltpu.roll(into_r, TILE - 1, 0))
        into_a = jnp.where(last, 0.0, pltpu.roll(into_a, TILE - 1, 0))
        into_m = jnp.where(last, 1.0, pltpu.roll(into_m, TILE - 1, 0))

    def scan(step, carried):
        value_next, sum_r, sum_a, tail, totals = carried
        at, value, carry_on, reward_in, delta = terms(LANES - 1 - step, value_next)
        sum_r = reward_in + jnp.where(carry_on, GAMMA_RATE * sum_r, 0.0)
        sum_a = delta + jnp.where(carry_on, rate * sum_a, 0.0)
        tail = jnp.where(carry_on, rate * tail, 0.0)
        time_r[at, :] = sum_r
        time_a[at, :] = sum_a
        time_m[at, :] = tail
        more = (jnp.where(tail > 0.0, 1.0, 0.0), sum_a, sum_a * sum_a, sum_a * tail, tail, tail * tail)
        return value, sum_r, sum_a, tail, tuple(t + m for t, m in zip(totals, more))

    _, head_r, head_a, _, totals = lax.fori_loop(
        0, LANES, scan, (nought, into_r, into_a, into_m, (nought,) * 6), unroll=8
    )
    head_a = head_a + first_value * (GAMMA_RATE / rate)
    send_z[...] = jnp.concatenate(
        [head_r[:1], head_a[:1]] + [jnp.sum(total, axis=0, keepdims=True) for total in totals],
        axis=0,
    )
    recv_z[tm] = send_z[...]

    order = lax.broadcasted_iota(jnp.int32, (height, height), 0) == jnp.broadcast_to(
        grp_ref[...], (height, height)
    )
    order = jnp.where(order, 1.0, 0.0).astype(BF16)
    twice = jnp.concatenate([order, order], axis=1)
    thrice = jnp.concatenate([order, order, order], axis=1)
    wide = 2 * LANES

    def permute(c, _):
        cols = pl.ds(pl.multiple_of(c * wide, wide), wide)
        for n, source in enumerate((time_r, time_a)):
            parts = [
                source[pl.ds(pl.multiple_of((2 * c + h) * STRIDE, TILE), LANES), :] for h in (0, 1)
            ]
            pieces = jnp.concatenate(split(jnp.concatenate(parts, axis=0), 2), axis=1)
            moved = lax.dot_general(
                twice, pieces, (((1,), (1,)), ((), ())), preferred_element_type=F32
            )
            send_bulk[:, n * TILE : (n + 1) * TILE, cols] = moved.reshape(n_batch, TILE, wide)
        return 0


    @pl.when(core == 0)
    def _():
        pl.semaphore_wait(barrier, 2 * n_batch - 1)
        pl.semaphore_signal(
            ready_sem, inc=1, device_id={"tm": partner, "batch": me}, device_id_type=MESH
        )

    @pl.when(core == 1)
    def _():
        pl.semaphore_wait(ready_sem, 1)

    def bulk(to, slot):
        return pltpu.make_async_remote_copy(
            src_ref=send_bulk.at[to],
            dst_ref=recv_bulk.at[slot],
            send_sem=bulk_ss.at[to],
            recv_sem=bulk_rs.at[slot],
            device_id={"tm": tm, "batch": to},
            device_id_type=MESH,
        )

    def send_one(d, _):
        bulk(lax.rem(me + d, n_batch), me).start()
        return 0

    def send_all():
        lax.fori_loop(0, span // wide, permute, 0)
        lax.fori_loop(1, n_batch, send_one, 0)

    @pl.when(tm < n_tm // 2)
    def _():
        send_all()

    @pl.when(core == 1)
    def _():
        pl.semaphore_wait(barrier, n_tm - 1)
        pl.semaphore_signal(
            ready_sem, inc=1, device_id={"tm": partner, "batch": me}, device_id_type=MESH
        )

    @pl.when(core == 0)
    def _():
        pl.semaphore_wait(ready_sem, 1)

    def along(to, slot):
        return pltpu.make_async_remote_copy(
            src_ref=send_z,
            dst_ref=recv_z.at[slot],
            send_sem=z_ss.at[to],
            recv_sem=z_rs.at[slot],
            device_id={"tm": to, "batch": me},
            device_id_type=MESH,
        )

    def tell_one(d, _):
        along(lax.rem(tm + d, n_tm), tm).start()
        return 0

    lax.fori_loop(1, n_tm, tell_one, 0)
    @pl.when(tm >= n_tm // 2)
    def _():
        send_all()

    recv_bulk[me] = send_bulk[me]

    def hear_one(d, _):
        along(lax.rem(tm + d, n_tm), lax.rem(tm + d, n_tm)).wait_recv()
        return 0

    lax.fori_loop(1, n_tm, hear_one, 0)

    lengths_f = lengths_row.astype(F32)
    whole_a = squarings(second_rate(lengths_f), 10)[10]
    whole_r = GAMMA_RATE**span
    whole_a = jnp.broadcast_to(whole_a, (TILE, LANES))
    zero = whole_a * 0.0

    def chain(k, carried):
        block = n_tm - 1 - k
        into_r, into_a, own_r, own_a, first, second = carried
        tile = recv_z[block]
        piece = [jnp.broadcast_to(tile[n : n + 1], (TILE, LANES)) for n in range(TILE)]
        mine = jnp.where(block == tm, 1.0, 0.0)
        own_r = own_r + mine * into_r
        own_a = own_a + mine * into_a
        first = first + piece[3] + piece[6] * into_a
        second = second + piece[4] + into_a * (2.0 * piece[5] + piece[7] * into_a)
        whole = piece[2] == float(span)
        into_r = piece[0] + jnp.where(whole, whole_r, 0.0) * into_r
        into_a = piece[1] + jnp.where(whole, whole_a, 0.0) * into_a
        return into_r, into_a, own_r, own_a, first, second

    _, _, own_r, own_a, first, second = lax.fori_loop(0, n_tm, chain, (zero,) * 6)
    lines = jnp.concatenate(
        [line[:1] for line in (own_r, own_a, first, second, send_z[2:3], lengths_f)]
        + [lengths_f - start.astype(F32), jnp.zeros((height - 7, LANES), F32)],
        axis=0,
    )
    send_stat[...] = lax.dot_general(
        thrice,
        jnp.concatenate(split(lines, 3), axis=1),
        (((1,), (1,)), ((), ())),
        preferred_element_type=F32,
    )
    recv_stat[me] = send_stat[pl.ds(pl.multiple_of(me * TILE, TILE), TILE), :]

    def stat(to, slot):
        return pltpu.make_async_remote_copy(
            src_ref=send_stat.at[pl.ds(pl.multiple_of(to * TILE, TILE), TILE), :],
            dst_ref=recv_stat.at[slot],
            send_sem=stat_ss.at[to],
            recv_sem=stat_rs.at[slot],
            device_id={"tm": tm, "batch": to},
            device_id_type=MESH,
        )

    def send_stats(d, _):
        stat(lax.rem(me + d, n_batch), me).start()
        return 0

    lax.fori_loop(1, n_batch, send_stats, 0)

    own_into = jnp.broadcast_to(own_a[:1], (LANES, LANES))
    for j in range(count):
        rows = pl.ds(j * STRIDE, LANES)
        own_out[:, j * LANES : (j + 1) * LANES] = (time_a[rows, :] + time_m[rows, :] * own_into).T
    def hear_stats(d, _):
        slot = lax.rem(me + d, n_batch)
        stat(slot, slot).wait_recv()
        return 0

    lax.fori_loop(1, n_batch, hear_stats, 0)
    def sent(d, _):
        to = lax.rem(me + d, n_batch)
        bulk(to, to).wait_recv()
        bulk(to, me).wait_send()
        stat(to, me).wait_send()
        return 0

    lax.fori_loop(1, n_batch, sent, 0)

    def told(d, _):
        along(lax.rem(tm + d, n_tm), tm).wait_send()
        return 0

    lax.fori_loop(1, n_tm, told, 0)


def finish(own, bulk, stats, adv_out, gadv_out, gret_out, held, done_r, done_a, out_sem):
    n_batch = bulk.shape[0]
    span = bulk.shape[2]
    count = span // LANES
    own_copy = pltpu.make_async_copy(own, adv_out, out_sem.at[0])
    own_copy.start()
    total = stats[0]
    for i in range(1, n_batch):
        total = total + stats[i]
    counted = total[:, 5:6]
    mean = total[:, 2:3] / counted
    var = total[:, 3:4] / counted - mean * mean
    mean = jnp.broadcast_to(mean, (TILE, LANES))
    inverse = jnp.broadcast_to(1.0 / jnp.sqrt(var + EPSILON), (TILE, LANES))
    lane = lax.broadcasted_iota(jnp.int32, (TILE, LANES), 1)
    lane_f = lane.astype(F32)
    gamma_powers = [GAMMA_RATE ** (1 << bit) for bit in range(8)]
    for i in range(n_batch):
        facts = stats[i]
        into_r, into_a, opened, lengths, limit = [
            jnp.broadcast_to(facts[:, n : n + 1], (TILE, LANES)) for n in (0, 1, 4, 5, 6)
        ]
        powers = squarings(second_rate(lengths), 7)
        scale = powers[7] / lane_powers(powers[:7], lane)
        held[0, i] = into_r
        held[1, i] = into_a * scale
        held[2, i] = powers[7]
        held[3, i] = float(span - 1) - opened
        held[4, i] = limit

    def stores(j):
        cols = pl.ds(pl.multiple_of(j * LANES, LANES), LANES)
        return [
            pltpu.make_async_copy(source.at[j], target.at[:, cols], out_sem.at[1 + 2 * j + n])
            for n, (source, target) in enumerate(((done_r, gret_out), (done_a, gadv_out)))
        ]

    def column(step, scale_r):
        j = count - 1 - step
        cols = pl.ds(pl.multiple_of(j * LANES, LANES), LANES)
        place = lane_f + (j * LANES).astype(F32)
        for i in range(n_batch):
            carried = place > held[3, i]
            more = held[1, i]
            ret = bulk[i, :TILE, cols] + jnp.where(carried, scale_r, 0.0) * held[0, i]
            adv = bulk[i, TILE:, cols] + jnp.where(carried, more, 0.0)
            held[1, i] = more * held[2, i]
            rows = pl.ds(i, TILE, stride=n_batch)
            done_r[j, rows, :] = ret
            done_a[j, rows, :] = jnp.where(place < held[4, i], (adv - mean) * inverse, 0.0)
        for copy in stores(j):
            copy.start()
        return scale_r * gamma_powers[7]

    lax.fori_loop(0, count, column, gamma_powers[7] / lane_powers(gamma_powers[:7], lane))
    own_copy.wait()
    for j in range(count):
        for copy in stores(j):
            copy.wait()


def solution(mesh):
    n_tm, n_batch = mesh.shape["tm"], mesh.shape["batch"]

    def on_device(rewards, values, episode_ends, lengths, groups):
        height, span = rewards.shape
        block = pltpu.VMEM((height, span), F32)
        square = pltpu.VMEM((height, LANES), F32)
        turned = pltpu.VMEM((TILE * STRIDE, LANES), F32)
        out = jax.ShapeDtypeStruct((height, span), F32)

        def kernel(*refs):
            fused(n_tm, n_batch, *refs)

        own, bulk, stats = pl.pallas_call(
            kernel,
            out_shape=(
                pltpu.VMEM((height, span), F32),
                pltpu.VMEM((n_batch, 2 * TILE, span), F32),
                pltpu.VMEM((n_batch, TILE, LANES), F32),
            ),
            in_specs=[pl.BlockSpec(memory_space=pltpu.VMEM)] * 2
            + [pl.BlockSpec(memory_space=pl.ANY)] * 3,
            out_specs=[pl.BlockSpec(memory_space=pltpu.VMEM)] * 3,
            scratch_shapes=[
                block,
                block,
                pltpu.VMEM((height, span), jnp.int32),
                turned,
                turned,
                pltpu.VMEM((TILE * STRIDE, LANES), jnp.int32),
                turned,
                turned,
                turned,
                pltpu.VMEM((n_batch, 2 * TILE, span), F32),
                pltpu.VMEM((TILE, LANES), F32),
                pltpu.VMEM((n_tm, TILE, LANES), F32),
                square,
                pltpu.SemaphoreType.DMA((4, 3)),
                pltpu.SemaphoreType.DMA((n_batch,)),
                pltpu.SemaphoreType.DMA((n_batch,)),
                pltpu.SemaphoreType.DMA((n_tm,)),
                pltpu.SemaphoreType.DMA((n_tm,)),
                pltpu.SemaphoreType.DMA((n_batch,)),
                pltpu.SemaphoreType.DMA((n_batch,)),
                pltpu.SemaphoreType.REGULAR,
            ],
            compiler_params=pltpu.CompilerParams(collective_id=0, has_side_effects=True),
        )(lengths.reshape(1, height), groups.reshape(1, height), rewards, values, episode_ends)
        columns = pltpu.VMEM((span // LANES, height, LANES), F32)
        return pl.pallas_call(
            finish,
            out_shape=(out, out, out),
            in_specs=[pl.BlockSpec(memory_space=pltpu.VMEM)] * 3,
            out_specs=[pl.BlockSpec(memory_space=pl.ANY)] * 3,
            scratch_shapes=[
                pltpu.VMEM((5, n_batch, TILE, LANES), F32),
                columns,
                columns,
                pltpu.SemaphoreType.DMA((1 + 2 * (span // LANES),)),
            ],
        )(*[pltpu.with_memory_space_constraint(a, pltpu.VMEM) for a in (own, bulk, stats)])

    return jax.shard_map(
        on_device,
        mesh=mesh,
        in_specs=(
            P("batch", "tm"),
            P("batch", "tm"),
            P("batch", "tm"),
            P("batch"),
            P("batch"),
        ),
        out_specs=(P("batch", "tm"), P("batch", "tm"), P("batch", "tm")),
        check_vma=False,
    )
```

time: 54.1 us -> 36.5 us (0.67)
  Pallas kernels: 49.2 us -> 35.7 us
  local copies, waits for them, and re-layouts: 3.97 us -> 0 us
    pallas_call x1 -> x2, Pallas kernels: 49.2 us -> 35.7 us  [the longest x1 34.2 us: on_device(): pl.pallas_call(kernel, out_shape=(pltpu.VMEM((height, span), F32), pltpu....]
    unnamed x7 -> x0, local copies, waits for them, and re-layouts: 3.97 us -> none
where the time goes in v2:
time: 36.5 us; the launch traced here: 36.3 us
  Pallas kernels  35.7 us (98%)
  between operations  0.64 us (2%)
    pallas_call x1, Pallas kernels, on_device(): pl.pallas_call(kernel, out_shape=(pltpu.VMEM((height, span), F32), pltpu....  34.2 us
    pallas_call x1, Pallas kernels, on_device(): pl.pallas_call(finish, out_shape=(out, out, out), in_specs=[pl.BlockSpec(...  1.52 us

profile of v2, /device:TPU:1, one launch (start us, length us, event | category | flops | bytes accessed | tf_op | source)
XLA Modules:
  0.0 36.3 jit_solution(8057757174144951769)
XLA Ops:
  0.6 34.2 %shard_map.76 = (f32[128,1024]{1,0:T(8,128)S(1)}, f32[16,16,1024]{2,1,0:T(8,128)S(1)}, f32[16,8,128]{2,1,0:T(8,128)S(1)}) custom-call(s32[1,128]{1,0:T(1,128)} %bitcast.2, s32[1,128]{1,0:T(1,128)} %bitcast.3, f32[128,1024]{1,0:T(8,128)} %refs_2_.1, f32[128,1024]{1,0:T(8,128)} %refs_3_.1, s32[128,1024]{1,0:T(8,128)} %refs_4_.1), custom_call_target="tpu_custom_call" | custom-call | tf_op jit(solution)/shard_map/pallas_call | solution.py:436
  34.8 1.5 %shard_map.77 = (f32[128,1024]{1,0:T(8,128)}, f32[128,1024]{1,0:T(8,128)}, f32[128,1024]{1,0:T(8,128)}) custom-call(f32[128,1024]{1,0:T(8,128)S(1)} %get-tuple-element.6.own, f32[16,16,1024]{2,1,0:T(8,128)S(1)} %get-tuple-element.7.bulk, f32[16,8,128]{2,1,0:T(8,128)S(1)} %get-tuple-element.8.stats), custom_call_target="tpu_custom_call" | custom-call | tf_op jit(solution)/shard_map/pallas_call | solution.py:472

commit v3 on v2

--- a/solution.py
+++ b/solution.py
@@ -1,3 +1,5 @@
+import math
+
 import jax
 import jax.numpy as jnp
 from jax import lax
@@ -47,14 +49,16 @@
 def fused(
     n_tm,
     n_batch,
-    len_ref,
-    grp_ref,
+    len_hbm,
+    grp_hbm,
     rew_hbm,
     val_hbm,
     end_hbm,
     own_out,
     recv_bulk,
     recv_stat,
+    len_ref,
+    grp_ref,
     rew,
     val,
     end,
@@ -68,7 +72,12 @@
     send_z,
     recv_z,
     send_stat,
+    send_pair,
+    recv_pair,
     in_sem,
+    small_sem,
+    pair_ss,
+    pair_rs,
     bulk_ss,
     bulk_rs,
     z_ss,
@@ -86,6 +95,18 @@
     core = lax.rem(tm, 2)
     partner = tm + 1 - 2 * core
     start = tm * span
+    chip = lax.div(tm, 2)
+    n_chips = n_tm // 2
+    side = math.isqrt(n_batch)
+    row, column = lax.div(me, side), lax.rem(me, side)
+
+    def away(distance, around):
+        return min(distance, around - distance)
+
+    steps = [(dx, dy) for dx in range(side) for dy in range(side) if dx or dy]
+    steps.sort(key=lambda step: -away(step[0], side) - away(step[1], side))
+    others = [lax.rem(row + dx, side) * side + lax.rem(column + dy, side) for dx, dy in steps]
+    chip_steps = sorted(range(1, n_chips), key=lambda step: -away(step, n_chips))
 
     def loads(k):
         cols = pl.ds(k * chunk_cols, chunk_cols)
@@ -94,9 +115,15 @@
             for n, (source, target) in enumerate(((rew_hbm, rew), (val_hbm, val), (end_hbm, end)))
         ]
 
+    small = [
+        pltpu.make_async_copy(source, target, small_sem.at[n])
+        for n, (source, target) in enumerate(((len_hbm, len_ref), (grp_hbm, grp_ref)))
+    ]
     for k in range(chunks):
         for copy in loads(k):
             copy.start()
+    for copy in small:
+        copy.start()
 
     barrier = pltpu.get_barrier_semaphore()
     for d in range(1, n_batch):
@@ -117,8 +144,6 @@
         barrier, inc=1, device_id={"tm": partner, "batch": me}, device_id_type=MESH
     )
 
-    lengths_row = len_ref[...]
-
     for k in range(chunks):
         for copy in loads(k):
             copy.wait()
@@ -127,6 +152,9 @@
             for source, target in ((rew, time_rew), (val, time_val), (end, time_end)):
                 target[rows, :] = source[:, j * LANES : (j + 1) * LANES].T
 
+    for copy in small:
+        copy.wait()
+    lengths_row = len_ref[...]
     sublane = lax.broadcasted_iota(jnp.int32, (TILE, LANES), 0)
     lengths = jnp.broadcast_to(lengths_row, (TILE, LANES))
     limit = lengths - (start + sublane * LANES)
@@ -187,7 +215,6 @@
         [head_r[:1], head_a[:1]] + [jnp.sum(total, axis=0, keepdims=True) for total in totals],
         axis=0,
     )
-    recv_z[tm] = send_z[...]
 
     order = lax.broadcasted_iota(jnp.int32, (height, height), 0) == jnp.broadcast_to(
         grp_ref[...], (height, height)
@@ -232,17 +259,51 @@
             device_id_type=MESH,
         )
 
-    def send_one(d, _):
-        bulk(lax.rem(me + d, n_batch), me).start()
-        return 0
-
     def send_all():
-        lax.fori_loop(0, span // wide, permute, 0)
-        lax.fori_loop(1, n_batch, send_one, 0)
+        for to in others:
+            bulk(to, me).start()
+
+    pair = pltpu.make_async_remote_copy(
+        src_ref=send_z,
+        dst_ref=recv_pair,
+        send_sem=pair_ss,
+        recv_sem=pair_rs,
+        device_id={"tm": partner, "batch": me},
+        device_id_type=MESH,
+    )
+    pair.start()
+    lax.fori_loop(0, span // wide, permute, 0)
 
     @pl.when(tm < n_tm // 2)
     def _():
         send_all()
+
+    pair.wait()
+    lengths_f = lengths_row.astype(F32)
+    whole_a = jnp.broadcast_to(squarings(second_rate(lengths_f), 10)[10], (TILE, LANES))
+    whole_r = GAMMA_RATE**span
+    mine, theirs = send_z[...], recv_pair[...]
+
+    def pieces_of(tile):
+        return [jnp.broadcast_to(tile[n : n + 1], (TILE, LANES)) for n in range(TILE)]
+
+    early = pieces_of(jnp.where(core == 0, mine, theirs))
+    late = pieces_of(jnp.where(core == 0, theirs, mine))
+    early_open = jnp.where(early[2] == float(span), 1.0, 0.0)
+    late_open = jnp.where(late[2] == float(span), 1.0, 0.0)
+    late_r, late_a = late_open * whole_r, late_open * whole_a
+    joined = (
+        early[0] + early_open * whole_r * late[0],
+        early[1] + early_open * whole_a * late[1],
+        early_open * late_open,
+        late[3] + early[3] + early[6] * late[1],
+        late[4] + early[4] + late[1] * (2.0 * early[5] + early[7] * late[1]),
+        late[5] + late_a * (early[5] + early[7] * late[1]),
+        late[6] + early[6] * late_a,
+        late[7] + early[7] * late_a * late_a,
+    )
+    send_pair[...] = jnp.concatenate([line[:1] for line in joined], axis=0)
+    recv_z[chip] = send_pair[...]
 
     @pl.when(core == 1)
     def _():
@@ -257,19 +318,17 @@
 
     def along(to, slot):
         return pltpu.make_async_remote_copy(
-            src_ref=send_z,
+            src_ref=send_pair,
             dst_ref=recv_z.at[slot],
             send_sem=z_ss.at[to],
             recv_sem=z_rs.at[slot],
-            device_id={"tm": to, "batch": me},
+            device_id={"tm": 2 * to + core, "batch": me},
             device_id_type=MESH,
         )
 
-    def tell_one(d, _):
-        along(lax.rem(tm + d, n_tm), tm).start()
-        return 0
-
-    lax.fori_loop(1, n_tm, tell_one, 0)
+    for step in chip_steps:
+        along(lax.rem(chip + step, n_chips), chip).start()
+
     @pl.when(tm >= n_tm // 2)
     def _():
         send_all()
@@ -277,33 +336,32 @@
     recv_bulk[me] = send_bulk[me]
 
     def hear_one(d, _):
-        along(lax.rem(tm + d, n_tm), lax.rem(tm + d, n_tm)).wait_recv()
+        other = lax.rem(chip + d, n_chips)
+        along(other, other).wait_recv()
         return 0
 
-    lax.fori_loop(1, n_tm, hear_one, 0)
-
-    lengths_f = lengths_row.astype(F32)
-    whole_a = squarings(second_rate(lengths_f), 10)[10]
-    whole_r = GAMMA_RATE**span
-    whole_a = jnp.broadcast_to(whole_a, (TILE, LANES))
+    lax.fori_loop(1, n_chips, hear_one, 0)
+
+    both_r, both_a = whole_r * whole_r, whole_a * whole_a
     zero = whole_a * 0.0
 
     def chain(k, carried):
-        block = n_tm - 1 - k
+        block = n_chips - 1 - k
         into_r, into_a, own_r, own_a, first, second = carried
-        tile = recv_z[block]
-        piece = [jnp.broadcast_to(tile[n : n + 1], (TILE, LANES)) for n in range(TILE)]
-        mine = jnp.where(block == tm, 1.0, 0.0)
-        own_r = own_r + mine * into_r
-        own_a = own_a + mine * into_a
+        piece = pieces_of(recv_z[block])
+        here = jnp.where(block == chip, 1.0, 0.0)
+        own_r = own_r + here * into_r
+        own_a = own_a + here * into_a
         first = first + piece[3] + piece[6] * into_a
         second = second + piece[4] + into_a * (2.0 * piece[5] + piece[7] * into_a)
-        whole = piece[2] == float(span)
-        into_r = piece[0] + jnp.where(whole, whole_r, 0.0) * into_r
-        into_a = piece[1] + jnp.where(whole, whole_a, 0.0) * into_a
+        into_r = piece[0] + piece[2] * both_r * into_r
+        into_a = piece[1] + piece[2] * both_a * into_a
         return into_r, into_a, own_r, own_a, first, second
 
-    _, _, own_r, own_a, first, second = lax.fori_loop(0, n_tm, chain, (zero,) * 6)
+    _, _, own_r, own_a, first, second = lax.fori_loop(0, n_chips, chain, (zero,) * 6, unroll=4)
+    is_early = jnp.where(core == 0, 1.0, 0.0)
+    own_r = is_early * (late[0] + late_r * own_r) + (1.0 - is_early) * own_r
+    own_a = is_early * (late[1] + late_a * own_a) + (1.0 - is_early) * own_a
     lines = jnp.concatenate(
         [line[:1] for line in (own_r, own_a, first, second, send_z[2:3], lengths_f)]
         + [lengths_f - start.astype(F32), jnp.zeros((height - 7, LANES), F32)],
@@ -327,11 +385,8 @@
             device_id_type=MESH,
         )
 
-    def send_stats(d, _):
-        stat(lax.rem(me + d, n_batch), me).start()
-        return 0
-
-    lax.fori_loop(1, n_batch, send_stats, 0)
+    for to in others:
+        stat(to, me).start()
 
     own_into = jnp.broadcast_to(own_a[:1], (LANES, LANES))
     for j in range(count):
@@ -353,10 +408,10 @@
     lax.fori_loop(1, n_batch, sent, 0)
 
     def told(d, _):
-        along(lax.rem(tm + d, n_tm), tm).wait_send()
+        along(lax.rem(chip + d, n_chips), chip).wait_send()
         return 0
 
-    lax.fori_loop(1, n_tm, told, 0)
+    lax.fori_loop(1, n_chips, told, 0)
 
 
 def finish(own, bulk, stats, adv_out, gadv_out, gret_out, held, done_r, done_a, out_sem):
@@ -440,10 +495,11 @@
                 pltpu.VMEM((n_batch, 2 * TILE, span), F32),
                 pltpu.VMEM((n_batch, TILE, LANES), F32),
             ),
-            in_specs=[pl.BlockSpec(memory_space=pltpu.VMEM)] * 2
-            + [pl.BlockSpec(memory_space=pl.ANY)] * 3,
+            in_specs=[pl.BlockSpec(memory_space=pl.ANY)] * 5,
             out_specs=[pl.BlockSpec(memory_space=pltpu.VMEM)] * 3,
             scratch_shapes=[
+                pltpu.VMEM((1, height), jnp.int32),
+                pltpu.VMEM((1, height), jnp.int32),
                 block,
                 block,
                 pltpu.VMEM((height, span), jnp.int32),
@@ -455,13 +511,18 @@
                 turned,
                 pltpu.VMEM((n_batch, 2 * TILE, span), F32),
                 pltpu.VMEM((TILE, LANES), F32),
-                pltpu.VMEM((n_tm, TILE, LANES), F32),
+                pltpu.VMEM((n_tm // 2, TILE, LANES), F32),
                 square,
+                pltpu.VMEM((TILE, LANES), F32),
+                pltpu.VMEM((TILE, LANES), F32),
                 pltpu.SemaphoreType.DMA((4, 3)),
+                pltpu.SemaphoreType.DMA((2,)),
+                pltpu.SemaphoreType.DMA,
+                pltpu.SemaphoreType.DMA,
                 pltpu.SemaphoreType.DMA((n_batch,)),
                 pltpu.SemaphoreType.DMA((n_batch,)),
-                pltpu.SemaphoreType.DMA((n_tm,)),
-                pltpu.SemaphoreType.DMA((n_tm,)),
+                pltpu.SemaphoreType.DMA((n_tm // 2,)),
+                pltpu.SemaphoreType.DMA((n_tm // 2,)),
                 pltpu.SemaphoreType.DMA((n_batch,)),
                 pltpu.SemaphoreType.DMA((n_batch,)),
                 pltpu.SemaphoreType.REGULAR,

time: 36.5 us -> 31.4 us (0.86)
  the two profiles are of different devices: /device:TPU:1 before, /device:TPU:2 now
where the time goes in v3:
time: 31.4 us; the launch traced here: 31.3 us
  Pallas kernels  30.7 us (98%)
  between operations  0.64 us (2%)
    pallas_call x1, Pallas kernels, on_device(): pl.pallas_call(kernel, out_shape=(pltpu.VMEM((height, span), F32), pltpu....  29.1 us
    pallas_call x1, Pallas kernels, on_device(): pl.pallas_call(finish, out_shape=(out, out, out), in_specs=[pl.BlockSpec(...  1.52 us

profile of v3, /device:TPU:2, one launch (start us, length us, event | category | flops | bytes accessed | tf_op | source)
XLA Modules:
  0.0 31.3 jit_solution(11595990274834750988)
XLA Ops:
  0.6 29.1 %shard_map.76 = (f32[128,1024]{1,0:T(8,128)S(1)}, f32[16,16,1024]{2,1,0:T(8,128)S(1)}, f32[16,8,128]{2,1,0:T(8,128)S(1)}) custom-call(s32[1,128]{1,0:T(1,128)} %bitcast.2, s32[1,128]{1,0:T(1,128)} %bitcast.3, f32[128,1024]{1,0:T(8,128)} %refs_2_.1, f32[128,1024]{1,0:T(8,128)} %refs_3_.1, s32[128,1024]{1,0:T(8,128)} %refs_4_.1), custom_call_target="tpu_custom_call" | custom-call | tf_op jit(solution)/shard_map/pallas_call | solution.py:491
  29.8 1.5 %shard_map.77 = (f32[128,1024]{1,0:T(8,128)}, f32[128,1024]{1,0:T(8,128)}, f32[128,1024]{1,0:T(8,128)}) custom-call(f32[128,1024]{1,0:T(8,128)S(1)} %get-tuple-element.6.own, f32[16,16,1024]{2,1,0:T(8,128)S(1)} %get-tuple-element.7.bulk, f32[16,8,128]{2,1,0:T(8,128)S(1)} %get-tuple-element.8.stats), custom_call_target="tpu_custom_call" | custom-call | tf_op jit(solution)/shard_map/pallas_call | solution.py:533

commit v4 on v3

--- a/solution.py
+++ b/solution.py
@@ -35,6 +35,21 @@
         factor = jnp.where((exponent & (1 << bit)) != 0, power, 1.0)
         result = factor if result is None else result * factor
     return result
+
+
+def joined(early, late):
+    b_r, b_a, a_r, a_a, s_0, t_0, t_1, s_1, t_2 = early
+    return [
+        b_r + a_r * late[0],
+        b_a + a_a * late[1],
+        a_r * late[2],
+        a_a * late[3],
+        late[4] + s_0 + s_1 * late[1],
+        late[5] + t_0 + late[1] * (2.0 * t_1 + t_2 * late[1]),
+        late[6] + late[3] * (t_1 + t_2 * late[1]),
+        late[7] + s_1 * late[3],
+        late[8] + t_2 * late[3] * late[3],
+    ]
 
 
 def split(value, terms):
@@ -172,29 +187,6 @@
         delta = jnp.where(inside, reward_in + follow - value, 0.0)
         return at, value, carry_on, reward_in, delta
 
-    def heads(step, carried):
-        value_next, sum_r, sum_a, whole = carried
-        _, value, carry_on, reward_in, delta = terms(LANES - 1 - step, value_next)
-        sum_r = reward_in + jnp.where(carry_on, GAMMA_RATE * sum_r, 0.0)
-        sum_a = delta + jnp.where(carry_on, rate * sum_a, 0.0)
-        return value, sum_r, sum_a, jnp.where(carry_on, whole, 0.0)
-
-    nought = limit.astype(F32) * 0.0
-    first_value, head_r, head_a, whole = lax.fori_loop(
-        0, LANES, heads, (nought, nought, nought, nought + 1.0), unroll=8
-    )
-    head_a = head_a + first_value * (GAMMA_RATE / rate)
-    into_r = into_a = nought
-    into_m = jnp.where(sublane == TILE - 1, 1.0, nought)
-    for _ in range(TILE - 1):
-        into_r = head_r + whole * whole_seg_r * into_r
-        into_a = head_a + whole * whole_seg_a * into_a
-        into_m = whole * whole_seg_a * into_m
-        last = sublane == TILE - 1
-        into_r = jnp.where(last, 0.0, pltpu.roll(into_r, TILE - 1, 0))
-        into_a = jnp.where(last, 0.0, pltpu.roll(into_a, TILE - 1, 0))
-        into_m = jnp.where(last, 1.0, pltpu.roll(into_m, TILE - 1, 0))
-
     def scan(step, carried):
         value_next, sum_r, sum_a, tail, totals = carried
         at, value, carry_on, reward_in, delta = terms(LANES - 1 - step, value_next)
@@ -207,13 +199,30 @@
         more = (jnp.where(tail > 0.0, 1.0, 0.0), sum_a, sum_a * sum_a, sum_a * tail, tail, tail * tail)
         return value, sum_r, sum_a, tail, tuple(t + m for t, m in zip(totals, more))
 
-    _, head_r, head_a, _, totals = lax.fori_loop(
-        0, LANES, scan, (nought, into_r, into_a, into_m, (nought,) * 6), unroll=8
+    nought = limit.astype(F32) * 0.0
+    first_value, head_r, head_a, _, totals = lax.fori_loop(
+        0, LANES, scan, (nought, nought, nought, nought + 1.0, (nought,) * 6), unroll=8
     )
     head_a = head_a + first_value * (GAMMA_RATE / rate)
+    seg_open = jnp.where(totals[0] == float(LANES), 1.0, 0.0)
+    seg_r, seg_a = seg_open * whole_seg_r, seg_open * whole_seg_a
+    tiles = (head_r, head_a, seg_r, seg_a) + totals[1:] + (totals[0], seg_open)
+    done = None
+    into_r = into_a = nought
+    into_m = nought + 1.0
+    for j in reversed(range(TILE)):
+        segment = [jnp.broadcast_to(tile[j : j + 1], (TILE, LANES)) for tile in tiles]
+        if done is None:
+            done, opened, still_open = segment[:9], segment[9], segment[10]
+            continue
+        into_r = jnp.where(sublane == j, done[0], into_r)
+        into_a = jnp.where(sublane == j, done[1], into_a)
+        into_m = jnp.where(sublane == j, done[3], into_m)
+        done = joined(segment[:9], done)
+        opened = opened + still_open * segment[9]
+        still_open = still_open * segment[10]
     send_z[...] = jnp.concatenate(
-        [head_r[:1], head_a[:1]] + [jnp.sum(total, axis=0, keepdims=True) for total in totals],
-        axis=0,
+        [line[:1] for line in (done[0], done[1], opened, *done[4:])], axis=0
     )
 
     order = lax.broadcasted_iota(jnp.int32, (height, height), 0) == jnp.broadcast_to(
@@ -253,13 +262,25 @@
         return pltpu.make_async_remote_copy(
             src_ref=send_bulk.at[to],
             dst_ref=recv_bulk.at[slot],
-            send_sem=bulk_ss.at[to],
-            recv_sem=bulk_rs.at[slot],
+            send_sem=bulk_ss,
+            recv_sem=bulk_rs,
             device_id={"tm": tm, "batch": to},
             device_id_type=MESH,
         )
 
     def send_all():
+        left = LANES - lax.broadcasted_iota(jnp.int32, (LANES, LANES), 0)
+        scale_r = lane_powers([GAMMA_RATE ** (1 << bit) for bit in range(8)], left)
+        for j in range(TILE):
+            rows = pl.ds(j * STRIDE, LANES)
+            more_r, more_a, more_m = [
+                jnp.broadcast_to(tile[j : j + 1], (LANES, LANES)) for tile in (into_r, into_a, into_m)
+            ]
+            tail = time_m[rows, :]
+            time_r[rows, :] = time_r[rows, :] + jnp.where(tail > 0.0, scale_r, 0.0) * more_r
+            time_a[rows, :] = time_a[rows, :] + tail * more_a
+            time_m[rows, :] = tail * more_m
+        lax.fori_loop(0, span // wide, permute, 0)
         for to in others:
             bulk(to, me).start()
 
@@ -272,11 +293,22 @@
         device_id_type=MESH,
     )
     pair.start()
-    lax.fori_loop(0, span // wide, permute, 0)
+
 
     @pl.when(tm < n_tm // 2)
     def _():
         send_all()
+
+    @pl.when(core == 1)
+    def _():
+        pl.semaphore_wait(barrier, n_tm - 1)
+        pl.semaphore_signal(
+            ready_sem, inc=1, device_id={"tm": partner, "batch": me}, device_id_type=MESH
+        )
+
+    @pl.when(core == 0)
+    def _():
+        pl.semaphore_wait(ready_sem, 1)
 
     pair.wait()
     lengths_f = lengths_row.astype(F32)
@@ -287,41 +319,25 @@
     def pieces_of(tile):
         return [jnp.broadcast_to(tile[n : n + 1], (TILE, LANES)) for n in range(TILE)]
 
-    early = pieces_of(jnp.where(core == 0, mine, theirs))
-    late = pieces_of(jnp.where(core == 0, theirs, mine))
-    early_open = jnp.where(early[2] == float(span), 1.0, 0.0)
-    late_open = jnp.where(late[2] == float(span), 1.0, 0.0)
-    late_r, late_a = late_open * whole_r, late_open * whole_a
-    joined = (
-        early[0] + early_open * whole_r * late[0],
-        early[1] + early_open * whole_a * late[1],
-        early_open * late_open,
-        late[3] + early[3] + early[6] * late[1],
-        late[4] + early[4] + late[1] * (2.0 * early[5] + early[7] * late[1]),
-        late[5] + late_a * (early[5] + early[7] * late[1]),
-        late[6] + early[6] * late_a,
-        late[7] + early[7] * late_a * late_a,
-    )
-    send_pair[...] = jnp.concatenate([line[:1] for line in joined], axis=0)
+    def block_of(tile):
+        piece = pieces_of(tile)
+        whole = jnp.where(piece[2] == float(span), 1.0, 0.0)
+        return piece[:2] + [whole * whole_r, whole * whole_a] + piece[3:], whole
+
+    early, early_open = block_of(jnp.where(core == 0, mine, theirs))
+    late, late_open = block_of(jnp.where(core == 0, theirs, mine))
+    both = joined(early, late)
+    send_pair[...] = jnp.concatenate(
+        [line[:1] for line in (both[0], both[1], early_open * late_open, *both[4:])], axis=0
+    )
     recv_z[chip] = send_pair[...]
-
-    @pl.when(core == 1)
-    def _():
-        pl.semaphore_wait(barrier, n_tm - 1)
-        pl.semaphore_signal(
-            ready_sem, inc=1, device_id={"tm": partner, "batch": me}, device_id_type=MESH
-        )
-
-    @pl.when(core == 0)
-    def _():
-        pl.semaphore_wait(ready_sem, 1)
 
     def along(to, slot):
         return pltpu.make_async_remote_copy(
             src_ref=send_pair,
             dst_ref=recv_z.at[slot],
-            send_sem=z_ss.at[to],
-            recv_sem=z_rs.at[slot],
+            send_sem=z_ss,
+            recv_sem=z_rs,
             device_id={"tm": 2 * to + core, "batch": me},
             device_id_type=MESH,
         )
@@ -335,12 +351,15 @@
 
     recv_bulk[me] = send_bulk[me]
 
-    def hear_one(d, _):
-        other = lax.rem(chip + d, n_chips)
-        along(other, other).wait_recv()
-        return 0
-
-    lax.fori_loop(1, n_chips, hear_one, 0)
+    all_z = pltpu.make_async_remote_copy(
+        src_ref=recv_z.at[pl.ds(0, n_chips - 1)],
+        dst_ref=recv_z.at[pl.ds(0, n_chips - 1)],
+        send_sem=z_ss,
+        recv_sem=z_rs,
+        device_id={"tm": partner, "batch": me},
+        device_id_type=MESH,
+    )
+    all_z.wait_recv()
 
     both_r, both_a = whole_r * whole_r, whole_a * whole_a
     zero = whole_a * 0.0
@@ -360,8 +379,8 @@
 
     _, _, own_r, own_a, first, second = lax.fori_loop(0, n_chips, chain, (zero,) * 6, unroll=4)
     is_early = jnp.where(core == 0, 1.0, 0.0)
-    own_r = is_early * (late[0] + late_r * own_r) + (1.0 - is_early) * own_r
-    own_a = is_early * (late[1] + late_a * own_a) + (1.0 - is_early) * own_a
+    own_r = is_early * (late[0] + late[2] * own_r) + (1.0 - is_early) * own_r
+    own_a = is_early * (late[1] + late[3] * own_a) + (1.0 - is_early) * own_a
     lines = jnp.concatenate(
         [line[:1] for line in (own_r, own_a, first, second, send_z[2:3], lengths_f)]
         + [lengths_f - start.astype(F32), jnp.zeros((height - 7, LANES), F32)],
@@ -379,8 +398,8 @@
         return pltpu.make_async_remote_copy(
             src_ref=send_stat.at[pl.ds(pl.multiple_of(to * TILE, TILE), TILE), :],
             dst_ref=recv_stat.at[slot],
-            send_sem=stat_ss.at[to],
-            recv_sem=stat_rs.at[slot],
+            send_sem=stat_ss,
+            recv_sem=stat_rs,
             device_id={"tm": tm, "batch": to},
             device_id_type=MESH,
         )
@@ -392,26 +411,25 @@
     for j in range(count):
         rows = pl.ds(j * STRIDE, LANES)
         own_out[:, j * LANES : (j + 1) * LANES] = (time_a[rows, :] + time_m[rows, :] * own_into).T
-    def hear_stats(d, _):
-        slot = lax.rem(me + d, n_batch)
-        stat(slot, slot).wait_recv()
-        return 0
-
-    lax.fori_loop(1, n_batch, hear_stats, 0)
-    def sent(d, _):
-        to = lax.rem(me + d, n_batch)
-        bulk(to, to).wait_recv()
-        bulk(to, me).wait_send()
-        stat(to, me).wait_send()
-        return 0
-
-    lax.fori_loop(1, n_batch, sent, 0)
-
-    def told(d, _):
-        along(lax.rem(chip + d, n_chips), chip).wait_send()
-        return 0
-
-    lax.fori_loop(1, n_chips, told, 0)
+    all_stats = pltpu.make_async_remote_copy(
+        src_ref=recv_stat.at[pl.ds(0, n_batch - 1)],
+        dst_ref=recv_stat.at[pl.ds(0, n_batch - 1)],
+        send_sem=stat_ss,
+        recv_sem=stat_rs,
+        device_id={"tm": partner, "batch": me},
+        device_id_type=MESH,
+    )
+    all_bulk = pltpu.make_async_remote_copy(
+        src_ref=send_bulk.at[pl.ds(0, n_batch - 1)],
+        dst_ref=recv_bulk.at[pl.ds(0, n_batch - 1)],
+        send_sem=bulk_ss,
+        recv_sem=bulk_rs,
+        device_id={"tm": partner, "batch": me},
+        device_id_type=MESH,
+    )
+    all_stats.wait()
+    all_bulk.wait()
+    all_z.wait_send()
 
 
 def finish(own, bulk, stats, adv_out, gadv_out, gret_out, held, done_r, done_a, out_sem):
@@ -519,12 +537,12 @@
                 pltpu.SemaphoreType.DMA((2,)),
                 pltpu.SemaphoreType.DMA,
                 pltpu.SemaphoreType.DMA,
-                pltpu.SemaphoreType.DMA((n_batch,)),
-                pltpu.SemaphoreType.DMA((n_batch,)),
-                pltpu.SemaphoreType.DMA((n_tm // 2,)),
-                pltpu.SemaphoreType.DMA((n_tm // 2,)),
-                pltpu.SemaphoreType.DMA((n_batch,)),
-                pltpu.SemaphoreType.DMA((n_batch,)),
+                pltpu.SemaphoreType.DMA,
+                pltpu.SemaphoreType.DMA,
+                pltpu.SemaphoreType.DMA,
+                pltpu.SemaphoreType.DMA,
+                pltpu.SemaphoreType.DMA,
+                pltpu.SemaphoreType.DMA,
                 pltpu.SemaphoreType.REGULAR,
             ],
             compiler_params=pltpu.CompilerParams(collective_id=0, has_side_effects=True),

time: 31.4 us -> 30.5 us (0.971)
  Pallas kernels: 30.7 us -> 29.8 us
    pallas_call x1, Pallas kernels: 29.1 us -> 28.2 us  [on_device(): pl.pallas_call(kernel, out_shape=(pltpu.VMEM((height, span), F32), pltpu....]
where the time goes in v4:
time: 30.5 us; the launch traced here: 30.4 us
  Pallas kernels  29.8 us (98%)
  between operations  0.64 us (2%)
    pallas_call x1, Pallas kernels, on_device(): pl.pallas_call(kernel, out_shape=(pltpu.VMEM((height, span), F32), pltpu....  28.2 us
    pallas_call x1, Pallas kernels, on_device(): pl.pallas_call(finish, out_shape=(out, out, out), in_specs=[pl.BlockSpec(...  1.52 us

profile of v4, /device:TPU:2, one launch (start us, length us, event | category | flops | bytes accessed | tf_op | source)
XLA Modules:
  0.0 30.4 jit_solution(10353822479370325991)
XLA Ops:
  0.6 28.2 %shard_map.76 = (f32[128,1024]{1,0:T(8,128)S(1)}, f32[16,16,1024]{2,1,0:T(8,128)S(1)}, f32[16,8,128]{2,1,0:T(8,128)S(1)}) custom-call(s32[1,128]{1,0:T(1,128)} %bitcast.2, s32[1,128]{1,0:T(1,128)} %bitcast.3, f32[128,1024]{1,0:T(8,128)} %refs_2_.1, f32[128,1024]{1,0:T(8,128)} %refs_3_.1, s32[128,1024]{1,0:T(8,128)} %refs_4_.1), custom_call_target="tpu_custom_call" | custom-call | tf_op jit(solution)/shard_map/pallas_call | solution.py:509
  28.9 1.5 %shard_map.77 = (f32[128,1024]{1,0:T(8,128)}, f32[128,1024]{1,0:T(8,128)}, f32[128,1024]{1,0:T(8,128)}) custom-call(f32[128,1024]{1,0:T(8,128)S(1)} %get-tuple-element.6.own, f32[16,16,1024]{2,1,0:T(8,128)S(1)} %get-tuple-element.7.bulk, f32[16,8,128]{2,1,0:T(8,128)S(1)} %get-tuple-element.8.stats), custom_call_target="tpu_custom_call" | custom-call | tf_op jit(solution)/shard_map/pallas_call | solution.py:551

commit v5 on v4

--- a/solution.py
+++ b/solution.py
@@ -103,7 +103,7 @@
 ):
     height, span = rew.shape
     count = span // LANES
-    chunks = 4
+    chunks = 2
     chunk_cols = span // chunks
     tm = lax.axis_index("tm")
     me = lax.axis_index("batch")
@@ -465,7 +465,7 @@
     def stores(j):
         cols = pl.ds(pl.multiple_of(j * LANES, LANES), LANES)
         return [
-            pltpu.make_async_copy(source.at[j], target.at[:, cols], out_sem.at[1 + 2 * j + n])
+            pltpu.make_async_copy(source.at[j], target.at[:, cols], out_sem.at[1 + n])
             for n, (source, target) in enumerate(((done_r, gret_out), (done_a, gadv_out)))
         ]
 
@@ -488,9 +488,8 @@
 
     lax.fori_loop(0, count, column, gamma_powers[7] / lane_powers(gamma_powers[:7], lane))
     own_copy.wait()
-    for j in range(count):
-        for copy in stores(j):
-            copy.wait()
+    pltpu.make_async_copy(own, gret_out, out_sem.at[1]).wait()
+    pltpu.make_async_copy(own, gadv_out, out_sem.at[2]).wait()
 
 
 def solution(mesh):
@@ -533,7 +532,7 @@
                 square,
                 pltpu.VMEM((TILE, LANES), F32),
                 pltpu.VMEM((TILE, LANES), F32),
-                pltpu.SemaphoreType.DMA((4, 3)),
+                pltpu.SemaphoreType.DMA((2, 3)),
                 pltpu.SemaphoreType.DMA((2,)),
                 pltpu.SemaphoreType.DMA,
                 pltpu.SemaphoreType.DMA,
@@ -557,7 +556,7 @@
                 pltpu.VMEM((5, n_batch, TILE, LANES), F32),
                 columns,
                 columns,
-                pltpu.SemaphoreType.DMA((1 + 2 * (span // LANES),)),
+                pltpu.SemaphoreType.DMA((3,)),
             ],
         )(*[pltpu.with_memory_space_constraint(a, pltpu.VMEM) for a in (own, bulk, stats)])
 

time: 30.5 us -> 30.3 us (level)
  no operation moved by 1% of the time
where the time goes in v5:
time: 30.3 us; the launch traced here: 30.2 us
  Pallas kernels  29.6 us (98%)
  between operations  0.64 us (2%)
    pallas_call x1, Pallas kernels, on_device(): pl.pallas_call(kernel, out_shape=(pltpu.VMEM((height, span), F32), pltpu....  28.2 us
    pallas_call x1, Pallas kernels, on_device(): pl.pallas_call(finish, out_shape=(out, out, out), in_specs=[pl.BlockSpec(...  1.37 us

profile of v5, /device:TPU:2, one launch (start us, length us, event | category | flops | bytes accessed | tf_op | source)
XLA Modules:
  0.0 30.2 jit_solution(5362342827264486768)
XLA Ops:
  0.6 28.2 %shard_map.76 = (f32[128,1024]{1,0:T(8,128)S(1)}, f32[16,16,1024]{2,1,0:T(8,128)S(1)}, f32[16,8,128]{2,1,0:T(8,128)S(1)}) custom-call(s32[1,128]{1,0:T(1,128)} %bitcast.2, s32[1,128]{1,0:T(1,128)} %bitcast.3, f32[128,1024]{1,0:T(8,128)} %refs_2_.1, f32[128,1024]{1,0:T(8,128)} %refs_3_.1, s32[128,1024]{1,0:T(8,128)} %refs_4_.1), custom_call_target="tpu_custom_call" | custom-call | tf_op jit(solution)/shard_map/pallas_call | solution.py:508
  28.8 1.4 %shard_map.77 = (f32[128,1024]{1,0:T(8,128)}, f32[128,1024]{1,0:T(8,128)}, f32[128,1024]{1,0:T(8,128)}) custom-call(f32[128,1024]{1,0:T(8,128)S(1)} %get-tuple-element.6.own, f32[16,16,1024]{2,1,0:T(8,128)S(1)} %get-tuple-element.7.bulk, f32[16,8,128]{2,1,0:T(8,128)S(1)} %get-tuple-element.8.stats), custom_call_target="tpu_custom_call" | custom-call | tf_op jit(solution)/shard_map/pallas_call | solution.py:550
